TPU v7x, 1024 devices: a whole 8x8x8 slice. The times are simulated.
1024 devices in a mesh: pipe: 8 (over z), dp: 4 (over x_lo, core), expert: 32 (over y, x_hi).
Axes of the slice: x: 8 (x_hi: 4, x_lo: 2; x = x_hi * 2 + x_lo), y: 8, z: 8, core: 2. Of those that a mesh axis runs over, the one named last changes fastest.
Arguments:
- cotangent: bfloat16 [8, 8192, 7168], P('pipe', ('dp', 'expert')), may hold values from -6 to 6
- routes: int32 [8, 2, 8192, 8], P('pipe', None, ('dp', 'expert')), may hold values from 0 to 255, as said below
- gates: bfloat16 [8, 2, 8192, 8], P('pipe', None, ('dp', 'expert')), may hold values from 0.099609375 to 1
- gate_pre: bfloat16 [8, 2, 4, 32, 2, 4096], P('pipe', None, 'dp', None, None, 'expert'), may hold values from -6 to 6
- up_pre: bfloat16 [8, 2, 4, 32, 2, 4096], P('pipe', None, 'dp', None, None, 'expert'), may hold values from -6 to 6
- w_gate: bfloat16 [8, 7168, 4096], P('pipe', None, 'expert'), may hold values from -0.0625 to 0.0625
- w_up: bfloat16 [8, 7168, 4096], P('pipe', None, 'expert'), may hold values from -0.0625 to 0.0625
- w_down: bfloat16 [8, 4096, 7168], P('pipe', 'expert'), may hold values from -0.125 to 0.125
Outputs:
- down_grad: float32 [8, 4096, 7168], P('pipe', 'expert', 'dp')
Inputs may be any that keep to these rules, and one draw needn't show every extreme that they name: `routes`: each token names 8 different experts. At one section and step the tokens of one device name each of the experts 0 to 1 at least once and at most 2 times; at every section and step, in some replica every device names one of them exactly 2 times.
All inputs are finite; a program needn't handle non-finite values.
Results may differ from a plain program's by a relative error of at most 0.0095.
Values may be sent and summed in bfloat16 or wider, within the bound.
A program may use at most 64 MiB of HBM per device.

v0:
```python
import jax
import jax.numpy as jnp
from jax import lax
from jax.sharding import PartitionSpec as P

EXP_FL = 2
STEPS = 2


def side_by_side(arrays, axis, split_dim, concat_dim, along):
    widths = [a.shape[along] for a in arrays]
    both = jnp.concatenate(arrays, axis=along)
    filled = lax.all_to_all(both, axis, split_axis=split_dim, concat_axis=concat_dim, tiled=True)
    return tuple(jnp.split(filled, [sum(widths[:k]) for k in range(1, len(widths))], axis=along))


def shifted(block, axis, distance):
    devices = range(lax.axis_size(axis))
    route = [(i - distance, i) for i in devices if i - distance in devices]
    return lax.ppermute(block, axis, route)


def split_up(value, dim, size):
    before, after = (value.shape[:dim], value.shape[dim + 1 :])
    return jnp.moveaxis(value.reshape(*before, size, -1, *after), dim, 0)


def sent_and_summed(value, axis, dim):
    pieces = split_up(value, dim, lax.axis_size(axis))
    arrived = lax.all_to_all(pieces, axis, split_axis=0, concat_axis=0, tiled=True)
    return arrived.astype(jnp.float32).sum(axis=0)


def slot_tables(ids, weights, capacity):
    match = (ids[:, :, None] == jnp.arange(EXP_FL, dtype=jnp.int32)).astype(jnp.float32)
    hit = jnp.sum(match, axis=1)
    gate_sum = jnp.sum(match * weights.astype(jnp.float32)[:, :, None], axis=1)
    rank = jnp.cumsum(hit, axis=0) - 1.0
    slots = jnp.arange(capacity, dtype=jnp.float32)
    select = hit[:, :, None] * (rank[:, :, None] == slots).astype(jnp.float32)
    select = jnp.transpose(select, (1, 2, 0)).reshape(EXP_FL * capacity, ids.shape[0])
    slot_gate = jnp.sum(
        select.reshape(EXP_FL, capacity, ids.shape[0]) * jnp.transpose(gate_sum)[:, None, :], axis=2
    )
    return (select, slot_gate)


def contract_last(left, right):
    return lax.dot_general(
        left, right, (((1,), (1,)), ((), ())), preferred_element_type=jnp.float32
    )


def contract_first(left, right):
    return lax.dot_general(
        left, right, (((0,), (0,)), ((), ())), preferred_element_type=jnp.float32
    )


def body(cotangent, routes, gates, gate_pre, up_pre, w_gate, w_up, w_down):
    n_shards = lax.axis_size("expert")
    split = n_shards // EXP_FL
    width = cotangent.shape[2]
    capacity = gate_pre.shape[4]
    hidden = gate_pre.shape[5]
    gate_mat = w_gate[0]
    up_mat = w_up[0]
    down_mat = w_down[0]
    owner = jnp.arange(n_shards) // split
    grad_in = cotangent[0]
    total = jnp.zeros((hidden, width), jnp.float32)
    for step in range(STEPS):
        select, slot_gate = slot_tables(routes[0, step], gates[0, step], capacity)
        rows = jnp.dot(
            select.astype(jnp.bfloat16), grad_in, preferred_element_type=jnp.float32
        ).astype(jnp.bfloat16)
        send_rows = rows.reshape(EXP_FL, capacity * width)[owner]
        send_gate = slot_gate.astype(jnp.bfloat16)[owner]
        got_rows, got_gate = side_by_side((send_rows, send_gate), "expert", 0, 0, 1)
        flat_rows = got_rows.reshape(n_shards * capacity, width)
        gate_col = got_gate.reshape(n_shards * capacity, 1).astype(jnp.float32)
        pre_u = gate_pre[0, step, 0].reshape(n_shards * capacity, hidden).astype(jnp.float32)
        pre_v = up_pre[0, step, 0].reshape(n_shards * capacity, hidden).astype(jnp.float32)
        grad_act = gate_col * contract_last(flat_rows, down_mat)
        sig = jax.nn.sigmoid(pre_u)
        act = pre_u * sig
        dsilu = sig * (1.0 + pre_u * (1.0 - sig))
        d_gate = (grad_act * pre_v * dsilu).astype(jnp.bfloat16)
        d_up = (grad_act * act).astype(jnp.bfloat16)
        scaled = (gate_col * act * pre_v).astype(jnp.bfloat16)
        total = total + contract_first(scaled, flat_rows)
        if step + 1 < STEPS:
            partial_value = contract_last(d_gate, gate_mat) + contract_last(d_up, up_mat)
            partial_value = partial_value.astype(jnp.bfloat16).reshape(n_shards, capacity * width)
            returned = lax.all_to_all(
                partial_value, "expert", split_axis=0, concat_axis=0, tiled=True
            )
            summed = jnp.sum(
                returned.astype(jnp.float32).reshape(EXP_FL, split, capacity * width), axis=1
            )
            summed = summed.reshape(EXP_FL * capacity, width)
            spread = contract_first(select, summed)
            grad_out = grad_in.astype(jnp.float32) + spread
            grad_in = shifted(grad_out.astype(jnp.bfloat16), "pipe", -1)
    reduced = sent_and_summed(total.astype(jnp.bfloat16), "dp", 1)
    return reduced[None]


def solution(mesh):
    in_specs = (
        P("pipe", ("dp", "expert"), None),
        P("pipe", None, ("dp", "expert"), None),
        P("pipe", None, ("dp", "expert"), None),
        P("pipe", None, "dp", None, None, "expert"),
        P("pipe", None, "dp", None, None, "expert"),
        P("pipe", None, "expert"),
        P("pipe", None, "expert"),
        P("pipe", "expert", None),
    )
    out_specs = P("pipe", "expert", "dp")
    return jax.shard_map(body, mesh=mesh, in_specs=in_specs, out_specs=out_specs, check_vma=False)
```

profile of v0, /device:TPU:1, one launch (start us, length us, event | category | flops | bytes accessed | tf_op | source)
XLA Modules:
  0.0 247.2 jit_solution(17265199240418869994)
XLA Ops:
  4.0 2.0 gather_fusion
  7.8 1.9 reduce
  9.8 3.5 %reshape.262 = bf16[32,2,7169]{2,1,0:T(2,128)(2,1)} reshape(bf16[32,14338]{1,0:T(8,128)(2,1)} %reduce) | data formatting | bytes 1835264
  13.3 13.6 %all-to-all-start = ((bf16[32,2,7169]{2,1,0:T(2,128)(2,1)}), bf16[32,2,7169]{2,1,0:T(2,128)(2,1)S(1)}, u32[]{:S(2)}, u32[]{:S(2)}) async-start(bf16[32,2,7169]{2,1,0:T(2,128)(2,1)} %reshape.262), calls=%async_computation | async-start | bytes 1867776 | tf_op jit(solution)/shard_map/all_to_all | solution.py:13
  26.9 31.0 %all-to-all-done = bf16[32,2,7169]{2,1,0:T(2,128)(2,1)S(1)} async-done(((bf16[32,2,7169]{2,1,0:T(2,128)(2,1)}), bf16[32,2,7169]{2,1,0:T(2,128)(2,1)S(1)}, u32[]{:S(2)}, u32[]{:S(2)}) %all-to-all-start) | async-done | bytes 917664 | tf_op jit(solution)/shard_map/all_to_all | solution.py:13
  57.9 2.4 reshape.263
  64.6 2.2 fusion.8
  70.1 3.8 %all_to_all.34 = bf16[32,1,14336]{2,1,0:T(2,128)(2,1)} reshape(bf16[64,7168]{1,0:T(8,128)(2,1)} %fusion.2) | data formatting | bytes 1835008 | tf_op jit(solution)/shard_map/all_to_all | solution.py:95
  73.9 8.1 %reduce.1 = bf16[32,14336]{1,0:T(8,128)(2,1)} reduce(bf16[32,1,14336]{2,1,0:T(2,128)(2,1)} %all_to_all.34, bf16[]{:T(256)} %broadcast.235), dimensions={1}, to_apply=%all_to_all.34.reduce_sub_computation | reduce | bytes 1835010 | tf_op jit(solution)/shard_map/all_to_all | solution.py:95
  81.9 3.5 %reshape.264 = bf16[32,2,7168]{2,1,0:T(2,128)(2,1)} reshape(bf16[32,14336]{1,0:T(8,128)(2,1)} %reduce.1) | data formatting | bytes 1835008
  85.5 32.9 %all_to_all.39 = bf16[32,2,7168]{2,1,0:T(2,128)(2,1)} all-to-all(bf16[32,2,7168]{2,1,0:T(2,128)(2,1)} %reshape.264), channel_id=1, replica_groups=mesh['pipe'=8,'dp'=4,'expert'=32] {'expert'}, dimensions={0} | all-to-all | bytes 1835008 | tf_op jit(solution)/shard_map/all_to_all | solution.py:95
  118.4 6.1 %reshape.265 = bf16[32,1,14336]{2,1,0:T(2,128)(2,1)} reshape(bf16[32,2,7168]{2,1,0:T(2,128)(2,1)} %all_to_all.39) | data formatting | bytes 1835008
  124.5 3.3 %copy.58 = f32[32,1,14336]{2,0,1:T(8,128)} copy(bf16[32,1,14336]{2,1,0:T(2,128)(2,1)} %reshape.265) | data formatting | bytes 2752512
  127.8 1.8 reduce_sum.76
  129.6 2.6 %fusion.1 = bf16[64,7168]{1,0:T(8,128)(2,1)} fusion(bf16[4,64]{1,0:T(4,128)(2,1)S(1)} %bitcast.88, bf16[4,7168]{1,0:T(4,128)(2,1)S(1)} %reshape.220, bf16[1,64,7168]{2,1,0:T(8,128)(2,1)} %param.8), kind=kOutput, calls=%fused_computation.8 | convolution fusion | flops 5046272 | bytes 1892864 | tf_op jit(solution)/shard_map/dot_general | solution.py:55
  134.5 24.9 %collective-permute-done = bf16[64,7168]{1,0:T(8,128)(2,1)} collective-permute-done((bf16[64,7168]{1,0:T(8,128)(2,1)}, bf16[64,7168]{1,0:T(8,128)(2,1)}, u32[]{:S(2)}, u32[]{:S(2)}) %collective-permute-start) | collective-permute-done | bytes 917536 | tf_op jit(solution)/shard_map/ppermute | solution.py:20
  161.0 2.0 gather_fusion.2
  163.0 2.2 maximum_bitcast_fusion.1
  165.2 3.1 %reduce.2 = bf16[32,14338]{1,0:T(8,128)(2,1)} reduce(bf16[32,1,14338]{2,0,1:T(8,128)(2,1)} %maximum_bitcast_fusion.1, bf16[]{:T(256)} %broadcast.235), dimensions={1}, to_apply=%copy.55.reduce_sub_computation | reduce | bytes 1835266 | tf_op jit(solution)/shard_map/all_to_all | solution.py:13
  168.3 3.5 %reshape.266 = bf16[32,2,7169]{2,1,0:T(2,128)(2,1)} reshape(bf16[32,14338]{1,0:T(8,128)(2,1)} %reduce.2) | data formatting | bytes 1835264
  171.8 34.3 %all_to_all.40 = bf16[32,2,7169]{2,1,0:T(2,128)(2,1)} all-to-all(bf16[32,2,7169]{2,1,0:T(2,128)(2,1)} %reshape.266), channel_id=1, replica_groups=mesh['pipe'=8,'dp'=4,'expert'=32] {'expert'}, dimensions={0} | all-to-all | bytes 1835264 | tf_op jit(solution)/shard_map/all_to_all | solution.py:13
  206.0 6.4 %reshape.267 = bf16[32,1,14338]{2,1,0:T(2,128)(2,1)} reshape(bf16[32,2,7169]{2,1,0:T(2,128)(2,1)} %all_to_all.40) | data formatting | bytes 1835264
  215.1 2.3 reshape.222
  219.5 26.4 %all_to_all.41 = bf16[4,128,1792]{2,1,0:T(8,128)(2,1)S(1)} all-to-all(bf16[4,128,1792]{2,1,0:T(8,128)(2,1)S(1)} %bitcast.71), channel_id=1, replica_groups=mesh['pipe'=8,'dp'=4,'expert'=32] {'dp'}, dimensions={0} | all-to-all | bytes 3670016 | tf_op jit(solution)/shard_map/all_to_all | solution.py:30
  (57 shorter events, 22.9 us)
Async XLA Ops:
  0.0 66.9 %copy-start = (bf16[1,7168,128]{2,1,0:T(8,128)(2,1)S(1)}, bf16[1,7168,128]{2,1,0:T(8,128)(2,1)}, u32[]{:S(2)}) copy-start(bf16[1,7168,128]{2,1,0:T(8,128)(2,1)} %param.13) | copy-start | bytes 5505028
  9.8 17.1 %copy-start.4 = (bf16[1,2,1,32,2,128]{5,4,3,2,1,0:T(2,128)(2,1)S(1)}, bf16[1,2,1,32,2,128]{5,4,3,2,1,0:T(2,128)(2,1)}, u32[]{:S(2)}) copy-start(bf16[1,2,1,32,2,128]{5,4,3,2,1,0:T(2,128)(2,1)} %param.11) | copy-start | bytes 98308
  9.8 17.1 %copy-start.3 = (bf16[1,2,1,32,2,128]{5,4,3,2,1,0:T(2,128)(2,1)S(1)}, bf16[1,2,1,32,2,128]{5,4,3,2,1,0:T(2,128)(2,1)}, u32[]{:S(2)}) copy-start(bf16[1,2,1,32,2,128]{5,4,3,2,1,0:T(2,128)(2,1)} %param.12) | copy-start | bytes 98308
  13.3 44.7 %all-to-all-start = ((bf16[32,2,7169]{2,1,0:T(2,128)(2,1)}), bf16[32,2,7169]{2,1,0:T(2,128)(2,1)S(1)}, u32[]{:S(2)}, u32[]{:S(2)}) async-start(bf16[32,2,7169]{2,1,0:T(2,128)(2,1)} %reshape.262), calls=%async_computation | async-start | bytes 1867776 | tf_op jit(solution)/shard_map/all_to_all | solution.py:13
  66.9 1.5 copy-start.2
  132.2 27.3 %collective-permute-start = (bf16[64,7168]{1,0:T(8,128)(2,1)}, bf16[64,7168]{1,0:T(8,128)(2,1)}, u32[]{:S(2)}, u32[]{:S(2)}) collective-permute-start(bf16[64,7168]{1,0:T(8,128)(2,1)} %fusion.1), channel_id=1, source_target_pairs={{128,0},{256,128},{384,256},{512,384},{640,512},{768,640},{896,768... | collective-permute-start | bytes 2752520 | tf_op jit(solution)/shard_map/ppermute | solution.py:20
  217.6 1.2 copy-start.1
where the time goes:
time: 251 us; the launch traced here: 247 us
  blocking collectives  93.6 us (37%)
  waiting for transfers between devices  55.9 us (22%)
  local copies, waits for them, and re-layouts  50.3 us (20%)
  other arithmetic  20.9 us (8%)
  starting transfers between devices  14.9 us (6%)
  matrix products  11.4 us (5%)
    all_to_all x1, blocking collectives, side_by_side(): lax.all_to_all(both, axis, split_axis=split_dim, concat_axis=concat_dim,...  34.3 us
    unnamed x19, local copies, waits for them, and re-layouts  33.2 us
    all_to_all x1, blocking collectives, body(): lax.all_to_all(partial_value, 'expert', split_axis=0, concat_axis=0, tile...  32.9 us
    all_to_all x1, waiting for transfers between devices, side_by_side(): lax.all_to_all(both, axis, split_axis=split_dim, concat_axis=concat_dim,...  31 us
    all_to_all x1, blocking collectives, sent_and_summed(): lax.all_to_all(pieces, axis, split_axis=0, concat_axis=0, tiled=True)  26.4 us
    ppermute x1, waiting for transfers between devices, shifted(): return lax.ppermute(block, axis, route)  24.9 us
    all_to_all x1, starting transfers between devices, side_by_side(): lax.all_to_all(both, axis, split_axis=split_dim, concat_axis=concat_dim,...  13.6 us
    all_to_all x4, other arithmetic, side_by_side(): lax.all_to_all(both, axis, split_axis=split_dim, concat_axis=concat_dim,...  8.46 us
  transfers between devices with their start and end apart: 2, of which 2 were waited for; matrix products, arithmetic and copies ran while one was open for 0% of the time, Pallas kernels for 0%

commit v1 on v0

v1 whole, which is shorter than its diff:
```python
import functools

import jax
import jax.numpy as jnp
from jax import lax
from jax.experimental import pallas as pl
from jax.experimental.pallas import tpu as pltpu
from jax.sharding import PartitionSpec as P

MESH = pl.DeviceIdType.MESH
BF = jnp.bfloat16
F32 = jnp.float32

D = 7168
TOK = 64
HID = 128
Q = 1792
H = 896
FAR = (4, 3, 5, 2, 6, 1, 7)
ROW = tuple((dx, dc) for dx in FAR for dc in (0, 1)) + ((0, 1),)


def dot(a, b, dims):
    return lax.dot_general(a, b, (dims, ((), ())), preferred_element_type=F32)


def one_hot_rows(source):
    i = lax.broadcasted_iota(jnp.int32, (128, 128), 0)
    j = lax.broadcasted_iota(jnp.int32, (128, 128), 1)
    return (source(i) == j).astype(F32).astype(BF)


def kernel(
    cot, routes, gates, gate_pre, up_pre, w_gate, w_up, w_down, out,
    g_v, ids_v, gat_v, w2, w13, sel_s, sel_in, rows_a, rows_b, base_v, m_out, uv, coef, perm, avt,
    xa, a2, yb, b2, ha, hb, dx, pa, pb, ra1, rb1, ta, tb, ra2, rb2, za, zb,
    ld, s_send, r_xa, r_yb, r_ha, r_hb, r_dx, r_ra1, r_rb1, r_ra2, r_rb2, r_uv, r_sel, r_base,
):
    p = lax.axis_index("pipe")
    r = lax.axis_index("dp")
    s = lax.axis_index("expert")
    y = s // 4
    x = (s % 4) * 2 + r // 2
    c = r % 2

    def dev(p_, x_, y_, c_):
        return (p_, (x_ % 2) * 2 + c_, y_ * 4 + x_ // 2)

    sends = []

    def send(src, dst, recv, target, like, when=None):
        k = len(sends)
        sends.append((like, when))
        pltpu.make_async_remote_copy(
            src_ref=src, dst_ref=dst, send_sem=s_send.at[k], recv_sem=recv, device_id=target, device_id_type=MESH
        ).start()

    def arrived(dst, recv):
        pltpu.make_async_copy(dst, dst, recv).wait()

    up = (p + 1) % 8
    down = (p + 7) % 8

    q0 = pl.multiple_of(r * Q, 128)
    loads = [
        pltpu.make_async_copy(routes.at[0], ids_v, ld.at[0]),
        pltpu.make_async_copy(gates.at[0], gat_v, ld.at[1]),
        pltpu.make_async_copy(cot.at[0], g_v, ld.at[2]),
        pltpu.make_async_copy(w_down.at[0, :, pl.ds(q0, Q)], w2, ld.at[3]),
        pltpu.make_async_copy(w_gate.at[0, pl.ds(q0, Q)], w13.at[:, 0:HID], ld.at[4]),
        pltpu.make_async_copy(w_up.at[0, pl.ds(q0, Q)], w13.at[:, HID : 2 * HID], ld.at[5]),
        pltpu.make_async_copy(gate_pre.at[0, :, 0], uv.at[r, 0], ld.at[6]),
        pltpu.make_async_copy(up_pre.at[0, :, 0], uv.at[r, 1], ld.at[7]),
    ]
    for cp in loads:
        cp.start()

    barrier = pltpu.get_barrier_semaphore()
    peers = [((x + dx_) % 8, y, (c + dc) % 2, p) for dx_, dc in ROW]
    peers += [(x, (y + dy) % 8, c, p) for dy in FAR]
    peers += [(x, y, c, up), (x, y, c, down)]
    for x_, y_, c_, p_ in peers:
        pl.semaphore_signal(barrier, inc=1, device_id=dev(p_, x_, y_, c_), device_id_type=MESH)

    loads[0].wait()
    loads[1].wait()
    lane = lax.broadcasted_iota(jnp.int32, (TOK, 128), 1)
    tri = (
        lax.broadcasted_iota(jnp.int32, (TOK, TOK), 0) >= lax.broadcasted_iota(jnp.int32, (TOK, TOK), 1)
    ).astype(F32).astype(BF)
    for t in range(2):
        ids = ids_v[t]
        gat = gat_v[t].astype(F32)
        hit = jnp.zeros((TOK, 128), F32)
        gsum = jnp.zeros((TOK, 128), F32)
        for e in range(2):
            match = (ids == e).astype(F32)
            mine = (lane >= 2 * e) & (lane < 2 * e + 2)
            hit = jnp.where(mine, jnp.sum(match, axis=1, keepdims=True), hit)
            gsum = jnp.where(mine, jnp.sum(match * gat, axis=1, keepdims=True), gsum)
        rank = dot(tri, hit.astype(BF), ((1,), (0,))) - 1.0
        slot = (lane & 1).astype(F32)
        sel = hit * (rank == slot).astype(F32)
        if t == 0:
            sel_s[0] = sel.astype(BF)
        sel_s[1 + t] = (sel * gsum).astype(BF)

    def put_rows(rows):
        for e in range(2):
            for q in range(4):
                rows_a[0, q, e] = rows[2 * e : 2 * e + 2, q * Q : q * Q + H].astype(BF)
                rows_b[0, e, :, q * H : (q + 1) * H] = rows[2 * e : 2 * e + 2, q * Q + H : (q + 1) * Q].astype(BF)

    loads[2].wait()
    put_rows(dot(sel_s[1], g_v[...], ((0,), (0,))))
    pl.semaphore_wait(barrier, len(peers))

    def first_stage(t):
        src = c * 8 + x
        for dx_, dc in ROW:
            x_, c_ = (x + dx_) % 8, (c + dc) % 2
            q_ = (x_ % 2) * 2 + c_
            send(rows_a.at[t, q_], xa.at[t, :, src], r_xa.at[t, src], dev(p, x_, y, c_), lambda: rows_a.at[0, 0])
        for dy in FAR:
            y_ = (y + dy) % 8
            send(rows_b.at[t, y_ // 4], yb.at[t, y], r_yb.at[t, y], dev(p, x, y_, c), lambda: rows_b.at[0, 0])
        xa[t, :, src] = rows_a[t, r]
        yb[t, y] = rows_b[t, y // 4]

    def second_a(t, k):
        for dx_ in FAR + (0,):
            i = k * 8 + (x + dx_) % 8
            if dx_ == 0:
                @pl.when(c != k)
                def _():
                    arrived(xa.at[t, :, i], r_xa.at[t, i])
            else:
                arrived(xa.at[t, :, i], r_xa.at[t, i])
        for e in range(2):
            a2[t, k, e] = xa[t, e, k * 8 : k * 8 + 8].reshape(16, H)
        for dy in FAR:
            y_ = (y + dy) % 8
            send(a2.at[t, k, y_ // 4], ha.at[t, k, y], r_ha.at[t, k, y], dev(p, x, y_, c), lambda: b2.at[0, 0])
        ha[t, k, y] = a2[t, k, y // 4]

    def second_b(t):
        for dy in FAR:
            y_ = (y + dy) % 8
            arrived(yb.at[t, y_], r_yb.at[t, y_])
        for q in range(4):
            b2[t, q] = yb[t, :, :, q * H : (q + 1) * H].reshape(16, H)

    def second_b_send(t, k):
        for dx_, dc in ROW:
            x_, c_ = (x + dx_) % 8, k if dc == 0 else 1 - k
            q_ = (x_ % 2) * 2 + c_
            send(b2.at[t, q_], hb.at[t, k, x], r_hb.at[t, k, x], dev(p, x_, y, c_), lambda: b2.at[0, 0], when=k)
        hb[t, k, x] = b2[t, r]

    def second_stage(t):
        for k in range(2):
            second_a(t, k)
            if k == 0:
                second_b(t)
            pl.when(c == k)(functools.partial(second_b_send, t, k))

    def dispatched(t, k):
        for dy in FAR:
            y_ = (y + dy) % 8
            arrived(ha.at[t, k, y_], r_ha.at[t, k, y_])
        for dx_ in FAR + (0,):
            x_ = (x + dx_) % 8
            if dx_ == 0:
                @pl.when(c != k)
                def _():
                    arrived(hb.at[t, k, x_], r_hb.at[t, k, x_])
            else:
                arrived(hb.at[t, k, x_], r_hb.at[t, k, x_])

    first_stage(0)
    send(sel_s.at[2], sel_in, r_sel, dev(up, x, y, c), lambda: sel_in)
    loads[6].wait()
    loads[7].wait()
    others = [(dxl, dc) for dxl in (0, 1) for dc in (0, 1) if (dxl, dc) != (0, 0)]

    def peer(dxl, dc):
        xl, c_ = (r // 2 + dxl) % 2, (c + dc) % 2
        return xl * 2 + c_

    for dxl, dc in others:
        send(uv.at[r], uv.at[r], r_uv.at[r], (p, peer(dxl, dc), s), lambda: uv.at[0])
    second_stage(0)

    arrived(sel_in, r_sel)
    base_v[...] = dot(sel_in[...], g_v[...], ((0,), (0,)))[0:8]
    m_out[...] = dot(sel_in[...], sel_s[0], ((0,), (0,)))[0:8]

    perm[0] = one_hot_rows(lambda i: ((i >> 1) & 1) * 64 + (i >> 4) * 8 + ((i >> 2) & 3) * 2 + (i & 1))
    perm[1] = one_hot_rows(lambda i: ((i >> 1) & 7) * 16 + (i >> 4) * 2 + (i & 1))
    for dxl, dc in others:
        i = peer(dxl, dc)
        arrived(uv.at[i], r_uv.at[i])
    for k in range(2):
        for t in range(2):
            u, v = (
                jnp.concatenate([uv[i, h, t].reshape(TOK, HID) for i in (k, 2 + k)], axis=0) for h in range(2)
            )
            both = dot(perm[0], jnp.concatenate([u, v], axis=1), ((1,), (0,)))
            u, v = both[:, 0:HID], both[:, HID : 2 * HID]
            sig = jax.nn.sigmoid(u)
            act = u * sig
            if t == 0:
                coef[k, 0] = v * (sig * (1.0 + u * (1.0 - sig)))
                coef[k, 1] = act
            av = (act * v).astype(BF)
            avt[0, :, t * 256 + k * 128 : t * 256 + k * 128 + 128] = av.astype(F32).T.astype(BF)
            avt[1, :, t * 256 + k * 128 : t * 256 + k * 128 + 128] = dot(perm[1], av, ((1,), (0,))).T.astype(BF)
    loads[3].wait()
    loads[4].wait()
    loads[5].wait()

    for k in range(2):
        dispatched(0, k)
        d_b = dot(hb[0, k].reshape(128, H), w2[:, H:Q], ((1,), (1,)))
        d_a = dot(ha[0, k].reshape(128, H), w2[:, 0:H], ((1,), (1,)))
        d_a = d_a + dot(perm[1], d_b.astype(BF), ((0,), (0,)))
        dx[k, r] = d_a.astype(BF)
        for dxl, dc in others:
            send(dx.at[k, r], dx.at[k, r], r_dx.at[k, r], (p, peer(dxl, dc), s), lambda: dx.at[0, 0])

    for k in range(2):
        for dxl, dc in others:
            i = peer(dxl, dc)
            arrived(dx.at[k, i], r_dx.at[k, i])
        d_act = (dx[k, 0].astype(F32) + dx[k, 1].astype(F32)) + (dx[k, 2].astype(F32) + dx[k, 3].astype(F32))
        d_gu = jnp.concatenate([(d_act * coef[k, 0]).astype(BF), (d_act * coef[k, 1]).astype(BF)], axis=1)
        pa[k] = dot(d_gu, w13[0:H, :], ((1,), (1,))).astype(BF).reshape(8, 16, H)
        for dy in FAR:
            y_ = (y + dy) % 8
            send(pa.at[k, y_], ra1.at[k, y], r_ra1.at[k, y], dev(p, x, y_, c), lambda: pa.at[0, 0])
        ra1[k, y] = pa[k, y]
        d_gu = dot(perm[1], d_gu, ((1,), (0,))).astype(BF)
        pb[k] = dot(d_gu, w13[H:Q, :], ((1,), (1,))).astype(BF).reshape(8, 16, H)

        def return_b(x_, when=None):
            send(pb.at[k, x_], rb1.at[r, s % 4], r_rb1.at[r, s % 4], dev(p, x_, y, k), lambda: pb.at[0, 0], when)

        for dx_ in FAR:
            return_b((x + dx_) % 8)
        pl.when(c != k)(functools.partial(return_b, x, 1 - k))

        @pl.when(c == k)
        def _():
            rb1[r, s % 4] = pb[k, x]

    for part in range(2):
        rows = (ha, hb)[part][0].reshape(256, H)
        out[0, :, part * H : (part + 1) * H] = dot(avt[part, :, 0:256], rows, ((1,), (0,)))

    def return_second_b():
        for q in range(4):
            acc = rb1[q, 0].astype(F32)
            for h in range(1, 4):
                acc = acc + rb1[q, h].astype(F32)
            tb[:, :, q * H : (q + 1) * H] = acc.astype(BF).reshape(8, 2, H)

    def wait_rb1():
        for dx_, dc in ROW:
            x_, c_ = (x + dx_) % 8, (c + dc) % 2
            q_ = (x_ % 2) * 2 + c_
            arrived(rb1.at[q_, x_ // 2], r_rb1.at[q_, x_ // 2])

    for k in range(2):
        for dy in FAR:
            y_ = (y + dy) % 8
            arrived(ra1.at[k, y_], r_ra1.at[k, y_])
        for e in range(2):
            acc = ra1[k, 4 * e].astype(F32)
            for h in range(1, 4):
                acc = acc + ra1[k, 4 * e + h].astype(F32)
            ta[k, :, e] = acc.astype(BF).reshape(8, 2, H)

        def return_a(x_, when=None):
            send(ta.at[k, x_], ra2.at[r, s % 4], r_ra2.at[r, s % 4], dev(p, x_, y, k), lambda: ta.at[0, 0], when)

        for dx_ in FAR:
            return_a((x + dx_) % 8)
        pl.when(c != k)(functools.partial(return_a, x, 1 - k))

        def own_chunk():
            ra2[r, s % 4] = ta[k, x]
            wait_rb1()
            return_second_b()
            for dy in FAR:
                y_ = (y + dy) % 8
                send(tb.at[y_], rb2.at[y], r_rb2.at[y], dev(p, x, y_, c), lambda: tb.at[0], k)
            rb2[y] = tb[y]

        pl.when(c == k)(own_chunk)

    alive = jnp.where(p > 0, 1.0, 0.0).astype(F32)
    mix = m_out[...] * alive

    def mixed(e, cols, back):
        acc = base_v[2 * e : 2 * e + 2, cols] * alive
        for f in range(2):
            for h in range(2):
                acc = acc + mix[2 * e : 2 * e + 2, 2 * f + h : 2 * f + h + 1] * back[f][h : h + 1, :]
        return acc.astype(BF)

    for dy in FAR:
        y_ = (y + dy) % 8
        arrived(rb2.at[y_], r_rb2.at[y_])
    back = []
    for f in range(2):
        acc = rb2[4 * f].astype(F32)
        for h in range(1, 4):
            acc = acc + rb2[4 * f + h].astype(F32)
        back.append(acc)
    for q in range(4):
        for e in range(2):
            zb[e, :, q * H : (q + 1) * H] = mixed(
                e, slice(q * Q + H, (q + 1) * Q), [b[:, q * H : (q + 1) * H] for b in back]
            )
    send(zb, rows_b.at[1], r_base.at[1], dev(down, x, y, c), lambda: zb)
    for dx_, dc in ROW:
        x_, c_ = (x + dx_) % 8, (c + dc) % 2
        q_ = (x_ % 2) * 2 + c_
        arrived(ra2.at[q_, x_ // 2], r_ra2.at[q_, x_ // 2])
    for q in range(4):
        back = []
        for f in range(2):
            acc = ra2[q, 0, f].astype(F32)
            for h in range(1, 4):
                acc = acc + ra2[q, h, f].astype(F32)
            back.append(acc)
        for e in range(2):
            za[q, e] = mixed(e, slice(q * Q, q * Q + H), back)
    send(za, rows_a.at[1], r_base.at[0], dev(down, x, y, c), lambda: za)
    arrived(rows_b.at[1], r_base.at[1])
    arrived(rows_a.at[1], r_base.at[0])

    first_stage(1)
    second_stage(1)
    for k in range(2):
        dispatched(1, k)
        for part in range(2):
            cols = slice(part * H, (part + 1) * H)
            rows = (ha, hb)[part][1, k].reshape(128, H)
            out[0, :, cols] += dot(avt[part, :, 256 + k * 128 : 384 + k * 128], rows, ((1,), (0,)))

    for k, (like, when) in enumerate(sends):
        def drained(like=like, k=k):
            pltpu.make_async_copy(like(), like(), s_send.at[k]).wait()

        if when is None:
            drained()
        else:
            pl.when(c == when)(drained)
    assert len(sends) <= N_SENDS, len(sends)


N_SENDS = 256


def body(*arguments):
    hbm = pl.BlockSpec(memory_space=pl.ANY)
    dma = pltpu.SemaphoreType.DMA
    return pl.pallas_call(
        kernel,
        out_shape=jax.ShapeDtypeStruct((1, HID, Q), F32),
        in_specs=[hbm] * 8,
        out_specs=pl.BlockSpec(memory_space=pltpu.VMEM),
        scratch_shapes=[
            pltpu.VMEM((TOK, D), BF),
            pltpu.VMEM((2, TOK, 8), jnp.int32),
            pltpu.VMEM((2, TOK, 8), BF),
            pltpu.VMEM((HID, Q), BF),
            pltpu.VMEM((Q, 2 * HID), BF),
            pltpu.VMEM((3, TOK, 128), BF),
            pltpu.VMEM((TOK, 128), BF),
            pltpu.VMEM((2, 4, 2, 2, H), BF),
            pltpu.VMEM((2, 2, 2, 4 * H), BF),
            pltpu.VMEM((8, D), F32),
            pltpu.VMEM((8, 128), F32),
            pltpu.VMEM((4, 2, 2, 32, 2, HID), BF),
            pltpu.VMEM((2, 2, 128, HID), F32),
            pltpu.VMEM((2, 128, 128), BF),
            pltpu.VMEM((2, HID, 512), BF),
            pltpu.VMEM((2, 2, 16, 2, H), BF),
            pltpu.VMEM((2, 2, 2, 16, H), BF),
            pltpu.VMEM((2, 8, 2, 4 * H), BF),
            pltpu.VMEM((2, 4, 16, H), BF),
            pltpu.VMEM((2, 2, 8, 16, H), BF),
            pltpu.VMEM((2, 2, 8, 16, H), BF),
            pltpu.VMEM((2, 4, 128, HID), BF),
            pltpu.VMEM((2, 8, 16, H), BF),
            pltpu.VMEM((2, 8, 16, H), BF),
            pltpu.VMEM((2, 8, 16, H), BF),
            pltpu.VMEM((4, 4, 16, H), BF),
            pltpu.VMEM((2, 8, 2, 2, H), BF),
            pltpu.VMEM((8, 2, 4 * H), BF),
            pltpu.VMEM((4, 4, 2, 2, H), BF),
            pltpu.VMEM((8, 2, 4 * H), BF),
            pltpu.VMEM((4, 2, 2, H), BF),
            pltpu.VMEM((2, 2, 4 * H), BF),
            dma((8,)),
            dma((N_SENDS,)),
            dma((2, 16)),
            dma((2, 8)),
            dma((2, 2, 8)),
            dma((2, 2, 8)),
            dma((2, 4)),
            dma((2, 8)),
            dma((4, 4)),
            dma((4, 4)),
            dma((8,)),
            dma((4,)),
            dma,
            dma((2,)),
        ],
        compiler_params=pltpu.CompilerParams(collective_id=0, has_side_effects=True),
        name="cooldown",
    )(*arguments)


def solution(mesh):
    in_specs = (
        P("pipe", ("dp", "expert"), None),
        P("pipe", None, ("dp", "expert"), None),
        P("pipe", None, ("dp", "expert"), None),
        P("pipe", None, "dp", None, None, "expert"),
        P("pipe", None, "dp", None, None, "expert"),
        P("pipe", None, "expert"),
        P("pipe", None, "expert"),
        P("pipe", "expert", None),
    )
    out_specs = P("pipe", "expert", "dp")
    return jax.shard_map(body, mesh=mesh, in_specs=in_specs, out_specs=out_specs, check_vma=False)
```

time: 251 us -> 87.9 us (0.35); the launches traced: 247 us -> 87.6 us
  blocking collectives: 93.6 us -> 0 us
  Pallas kernels: 0 us -> 82.7 us
  waiting for transfers between devices: 55.9 us -> 0 us
  local copies, waits for them, and re-layouts: 50.3 us -> 4.96 us
  other arithmetic: 20.9 us -> 0 us
  starting transfers between devices: 14.9 us -> 0 us
  matrix products: 11.4 us -> 0 us
    all_to_all x3 -> x0, blocking collectives: 93.6 us -> none  [the longest x1 34.3 us: side_by_side(): lax.all_to_all(both, axis, split_axis=split_dim, concat_axis=concat_dim,...]
    pallas_call x0 -> x1, Pallas kernels: none -> 82.7 us  [body(): pl.pallas_call(kernel, out_shape=jax.ShapeDtypeStruct((1, HID, Q), F32),...]
    all_to_all x1 -> x0, waiting for transfers between devices: 31 us -> none  [side_by_side(): lax.all_to_all(both, axis, split_axis=split_dim, concat_axis=concat_dim,...]
    unnamed x19 -> x3, local copies, waits for them, and re-layouts: 33.2 us -> 4.96 us
    ppermute x1 -> x0, waiting for transfers between devices: 24.9 us -> none  [shifted(): return lax.ppermute(block, axis, route)]
    all_to_all x5 -> x0, other arithmetic: 16.5 us -> none  [the longest x4 8.46 us: side_by_side(): lax.all_to_all(both, axis, split_axis=split_dim, concat_axis=concat_dim,...]
    all_to_all x1 -> x0, starting transfers between devices: 13.6 us -> none  [side_by_side(): lax.all_to_all(both, axis, split_axis=split_dim, concat_axis=concat_dim,...]
    dot_general x8 -> x0, matrix products: 11.4 us -> none  [the longest x3 4.68 us: contract_last(): lax.dot_general(left, right, (((1,), (1,)), ((), ())), preferred_element_...]
  transfers between devices with their start and end apart: 2 -> 0, of which waited for: 2 -> 0; matrix products, arithmetic and copies ran while one was open for 0% -> 0% of each run, Pallas kernels for 0% -> 0%
where the time goes in v1:
time: 87.9 us; the launch traced here: 87.6 us
  Pallas kernels  82.7 us (94%)
  local copies, waits for them, and re-layouts  4.96 us (6%)
    pallas_call x1, Pallas kernels, body(): pl.pallas_call(kernel, out_shape=jax.ShapeDtypeStruct((1, HID, Q), F32),...  82.7 us
    unnamed x3, local copies, waits for them, and re-layouts  4.96 us

profile of v1, /device:TPU:1, one launch (start us, length us, event | category | flops | bytes accessed | tf_op | source)
XLA Modules:
  0.0 87.6 jit_solution(11605770091257559983)
XLA Ops:
  0.0 1.4 %copy.10.gates = bf16[1,2,64,8]{3,2,1,0:T(8,128)(2,1)} copy(bf16[1,2,64,8]{2,3,1,0:T(8,128)(2,1)} %param.10) | data formatting | bytes 4096 | tf_op args[2]
  1.4 1.4 %copy.9.routes = s32[1,2,64,8]{3,2,1,0:T(8,128)} copy(s32[1,2,64,8]{2,3,1,0:T(8,128)} %param.9) | data formatting | bytes 8192 | tf_op args[1]
  2.8 82.7 %cooldown.1 = f32[1,128,1792]{2,1,0:T(8,128)} custom-call(bf16[1,64,7168]{2,1,0:T(8,128)(2,1)} %cot.1, s32[1,2,64,8]{3,2,1,0:T(8,128)} %copy.9.routes, bf16[1,2,64,8]{3,2,1,0:T(8,128)(2,1)} %copy.10.gates, bf16[1,2,1,32,2,128]{5,4,3,2,1,0:T(2,128)(2,1)} %gate_pre.1, bf16[1,2,1,32,2,128]{5,4,3,2,1,0:T(2,128)(2,1)} %up_pre.1, bf16[1,7168,128]{2,1,0:T(8,128)(2,1)} %w_gate.1, ...), custom_call_target="tpu_custom_call" | custom-call | tf_op jit(solution)/shard_map/cooldown/pallas_call | solution.py:369
  85.5 2.2 %copy.12 = f32[1,128,1792]{2,1,0:T(8,128)} copy(f32[1,128,1792]{2,1,0:T(8,128)} %cooldown.1) | data formatting | bytes 1835008

commit v2 on v0

v2 whole, which is shorter than its diff:
```python
import functools

import jax
import jax.numpy as jnp
from jax import lax
from jax.experimental import pallas as pl
from jax.experimental.pallas import tpu as pltpu
from jax.sharding import PartitionSpec as P

MESH = pl.DeviceIdType.MESH
BF = jnp.bfloat16
F32 = jnp.float32

D = 7168
TOK = 64
HID = 128
Q = 1792
H = 896
K = 4
FAR = (4, 3, 5, 2, 6, 1, 7)
ROW = tuple((dx, dc) for dx in FAR for dc in (0, 1)) + ((0, 1),)


def dot(a, b, dims):
    return lax.dot_general(a, b, (dims, ((), ())), preferred_element_type=F32)


def kernel(
    cot, routes, gates, gate_pre, up_pre, w_gate, w_up, w_down, out,
    g_v, ids_v, gat_v, w2, w13, sel_s, sel_in, rows_a, rows_b, base_v, base_o, base_in, m_v, m_in, uv, coef, perm, avt, total,
    xa, a2, yb, b2, ha, hb, hd, dx, pa, pb, ra1, rb1, ta, tb, ra2, rb2,
    ld, st, snd, r_xa, r_yb, r_ha, r_hb, r_dx, r_ra1, r_rb1, r_ra2, r_rb2, r_one,
):
    p = lax.axis_index("pipe")
    r = lax.axis_index("dp")
    s = lax.axis_index("expert")
    y = s // 4
    xh = s % 4
    x = xh * 2 + r // 2
    c = r % 2
    up = (p + 1) % 8
    down = (p + 7) % 8
    mine = (r + y) % 4
    half = y // 4

    def dev(p_, x_, y_, c_):
        return (p_, (x_ % 2) * 2 + c_, y_ * 4 + x_ // 2)

    def send(src, dst, kind, recv, target):
        pltpu.make_async_remote_copy(
            src_ref=src, dst_ref=dst, send_sem=snd.at[kind], recv_sem=recv, device_id=target, device_id_type=MESH
        ).start()

    def arrived(like, sem):
        pltpu.make_async_copy(like, like, sem).wait()

    D1A, D1B, D2A, D2B, DX, R1A, R1B, R2A, R2B, UV, SEL, BASE, MM, D1A1, D1B1 = range(15)

    barrier = pltpu.get_barrier_semaphore()
    peers = [((x + ox) % 8, y, (c + oc) % 2, p) for ox, oc in ROW]
    peers += [(x, (y + oy) % 8, c, p) for oy in FAR]
    peers += [(x, y, c, up), (x, y, c, down)]
    for x_, y_, c_, p_ in peers:
        pl.semaphore_signal(barrier, inc=1, device_id=dev(p_, x_, y_, c_), device_id_type=MESH)

    q0 = pl.multiple_of(r * Q, 128)
    loads = [
        pltpu.make_async_copy(routes.at[0], ids_v, ld.at[0]),
        pltpu.make_async_copy(gates.at[0], gat_v, ld.at[1]),
        pltpu.make_async_copy(cot.at[0], g_v, ld.at[2]),
        pltpu.make_async_copy(w_down.at[0, :, pl.ds(q0, Q)], w2, ld.at[3]),
        pltpu.make_async_copy(w_gate.at[0, pl.ds(q0, Q)], w13.at[:, 0:HID], ld.at[4]),
        pltpu.make_async_copy(w_up.at[0, pl.ds(q0, Q)], w13.at[:, HID : 2 * HID], ld.at[5]),
        pltpu.make_async_copy(gate_pre.at[0, :, 0], uv.at[r, 0], ld.at[6]),
        pltpu.make_async_copy(up_pre.at[0, :, 0], uv.at[r, 1], ld.at[7]),
    ]
    for cp in loads:
        cp.start()

    loads[0].wait()
    loads[1].wait()
    row = lax.broadcasted_iota(jnp.int32, (8, TOK), 0)
    upto = (
        lax.broadcasted_iota(jnp.int32, (TOK, TOK), 0) <= lax.broadcasted_iota(jnp.int32, (TOK, TOK), 1)
    ).astype(F32).astype(BF)
    for t in range(2):
        ids = ids_v[t]
        gat = gat_v[t].astype(F32)
        hit = jnp.zeros((8, TOK), F32)
        gsum = jnp.zeros((8, TOK), F32)
        for e in range(2):
            match = (ids == e).astype(F32)
            of_e = (row >= 2 * e) & (row < 2 * e + 2)
            hit = jnp.where(of_e, jnp.sum(match, axis=0, keepdims=True), hit)
            gsum = jnp.where(of_e, jnp.sum(match * gat, axis=0, keepdims=True), gsum)
        rank = dot(hit.astype(BF), upto, ((1,), (0,))) - 1.0
        sel = hit * (rank == (row & 1).astype(F32)).astype(F32)
        if t == 0:
            sel_s[0] = sel.astype(BF)
        sel_s[1 + t] = (sel * gsum).astype(BF)

    loads[2].wait()
    rows = dot(sel_s[1], g_v[...], ((1,), (0,)))
    for e in range(2):
        for q in range(4):
            rows_a[0, q, e] = rows[2 * e : 2 * e + 2, q * Q : q * Q + H].astype(BF)
            rows_b[0, e, :, q * H : (q + 1) * H] = rows[2 * e : 2 * e + 2, q * Q + H : (q + 1) * Q].astype(BF)

    pl.semaphore_wait(barrier, len(peers))

    def first_a(t):
        for ox, oc in ROW:
            x_, c_ = (x + ox) % 8, (c + oc) % 2
            q_ = (x_ % 2) * 2 + c_
            send(rows_a.at[t, q_], xa.at[t, mine, xh], (D1A, D1A1)[t], r_xa.at[t, mine], dev(p, x_, y, c_))
        xa[t, mine, xh] = rows_a[t, r]

    def first_b(t):
        for oy in FAR + (0,) * t:
            y_ = (y + oy) % 8
            send(
                rows_b.at[t, y_ // 4], yb.at[t, y % 4, half], (D1B, D1B1)[t], r_yb.at[t, mine], dev((p, down)[t], x, y_, c)
            )
        if t == 0:
            yb[t, y % 4, half] = rows_b[t, half]

    def second(t, k):
        @pl.when(mine == k)
        def _():
            arrived(xa.at[t, k, 0:3], r_xa.at[t, k])

        @pl.when(mine != k)
        def _():
            arrived(xa.at[t, k], r_xa.at[t, k])

        for e in range(2):
            a2[t, k, e] = jnp.concatenate([xa[t, k, h, e] for h in range(4)], axis=0)
        for oy in FAR:
            y_ = (y + oy) % 8
            send(a2.at[t, k, y_ // 4], ha.at[t, k, y], D2A, r_ha.at[t, k], dev(p, x, y_, c))
        ha[t, k, y] = a2[t, k, half]
        v = (k + 4 - r) % 4
        if t == 0:
            @pl.when(mine == k)
            def _():
                arrived(yb.at[t, k, 0], r_yb.at[t, k])

            @pl.when(mine != k)
            def _():
                arrived(yb.at[t, k], r_yb.at[t, k])
        else:
            arrived(yb.at[t, k], r_yb.at[t, k])
        for h in range(2):
            for q in range(4):
                b2[t, k, q, 2 * h : 2 * h + 2, :] = yb[t, v, h, :, q * H : (q + 1) * H]
        for ox, oc in ROW:
            x_, c_ = (x + ox) % 8, (c + oc) % 2
            q_ = (x_ % 2) * 2 + c_
            send(b2.at[t, k, q_], hb.at[t, k, r * 4 + xh], D2B, r_hb.at[t, k], dev(p, x_, y, c_))
        hb[t, k, r * 4 + xh] = b2[t, k, r]

    def dispatched(t, k):
        arrived(ha.at[t, k, 0:7], r_ha.at[t, k])
        arrived(hb.at[t, k, 0:15], r_hb.at[t, k])
        hd[t, k] = hb[t, k].reshape(64, H)

    others = [(ol, oc) for ol in (0, 1) for oc in (0, 1) if (ol, oc) != (0, 0)]

    def peer(ol, oc):
        return ((r // 2 + ol) % 2) * 2 + (c + oc) % 2

    first_a(0)
    first_b(0)
    send(sel_s.at[2], sel_in, SEL, r_one.at[0], dev(up, x, y, c))
    loads[6].wait()
    loads[7].wait()
    for ol, oc in others:
        send(uv.at[r], uv.at[r], UV, r_one.at[1], (p, peer(ol, oc), s))
    for k in range(K):
        second(0, k)

    arrived(sel_in, r_one.at[0])
    base_v[...] = dot(sel_in[...], g_v[...], ((1,), (0,)))
    m_v[...] = dot(sel_in[...], sel_s[0], ((1,), (1,)))
    for e in range(2):
        for q in range(4):
            base_o[q, e] = base_v[2 * e : 2 * e + 2, q * Q : q * Q + H]
    send(base_o, base_in, BASE, r_one.at[2], dev(down, x, y, c))
    send(m_v, m_in, MM, r_one.at[3], dev(down, x, y, c))

    arrived(uv.at[0:3], r_one.at[1])
    i64 = lax.broadcasted_iota(jnp.int32, (64, 64), 0)
    j64 = lax.broadcasted_iota(jnp.int32, (64, 64), 1)
    for k in range(K):
        src = ((((k + 4) - (i64 >> 4)) & 3) + ((i64 >> 1) & 1) * 4) * 8 + ((i64 >> 2) & 3) * 2 + (i64 & 1)
        perm[k] = (src == j64).astype(F32).astype(BF)
        for t in range(2):
            u, v = (
                jnp.concatenate(
                    [uv[(k - yy) % 4, h, t, 4 * yy : 4 * yy + 4].astype(F32).reshape(8, HID) for yy in range(8)], axis=0
                )
                for h in range(2)
            )
            sig = jax.nn.sigmoid(u)
            act = u * sig
            if t == 0:
                coef[k, 0] = v * (sig * (1.0 + u * (1.0 - sig)))
                coef[k, 1] = act
            av = (act * v).astype(BF)
            avt[0, t, k] = av.astype(F32).T.astype(BF)
            avt[1, t, k] = dot(perm[k], av, ((1,), (0,))).T.astype(BF)
    loads[3].wait()
    loads[4].wait()
    loads[5].wait()

    def hidden_gradient(k):
        dispatched(0, k)
        d_b = dot(hd[0, k], w2[:, H:Q], ((1,), (1,)))
        d_a = dot(ha[0, k].reshape(64, H), w2[:, 0:H], ((1,), (1,)))
        d_a = d_a + dot(perm[k], d_b.astype(BF), ((0,), (0,)))
        dx[k, r] = d_a.astype(BF)
        for ol, oc in others:
            send(dx.at[k, r], dx.at[k, r], DX, r_dx.at[k], (p, peer(ol, oc), s))

    def input_gradient(k):
        arrived(dx.at[k, 0:3], r_dx.at[k])
        d_act = (dx[k, 0].astype(F32) + dx[k, 1].astype(F32)) + (dx[k, 2].astype(F32) + dx[k, 3].astype(F32))
        d_gu = jnp.concatenate([(d_act * coef[k, 0]).astype(BF), (d_act * coef[k, 1]).astype(BF)], axis=1)
        pa[k] = dot(d_gu, w13[0:H, :], ((1,), (1,))).astype(BF).reshape(8, 8, H)
        for oy in FAR:
            y_ = (y + oy) % 8
            send(pa.at[k, y_], ra1.at[k, y], R1A, r_ra1.at[k], dev(p, x, y_, c))
        ra1[k, y] = pa[k, y]
        d_gu = dot(perm[k], d_gu, ((1,), (0,))).astype(BF)
        pb[k] = dot(d_gu, w13[H:Q, :], ((1,), (1,))).astype(BF).reshape(16, 4, H)
        for ox, oc in ROW:
            x_, c_ = (x + ox) % 8, (c + oc) % 2
            i_ = ((x_ % 2) * 2 + c_) * 4 + x_ // 2
            send(pb.at[k, i_], rb1.at[k, r * 4 + xh], R1B, r_rb1.at[k], dev(p, x_, y, c_))
        rb1[k, r * 4 + xh] = pb[k, r * 4 + xh]

    def to_sources(k):
        arrived(ra1.at[k, 0:7], r_ra1.at[k])
        for e in range(2):
            acc = ra1[k, 4 * e].astype(F32)
            for h in range(1, 4):
                acc = acc + ra1[k, 4 * e + h].astype(F32)
            for h in range(4):
                ta[k, h, e] = acc[2 * h : 2 * h + 2].astype(BF)
        r_ = (k + 8 - y) % 4
        for h in range(4):
            send(ta.at[k, h], ra2.at[r * 4 + xh], R2A, r_ra2, (down, r_, y * 4 + h))
        arrived(rb1.at[k, 0:15], r_rb1.at[k])
        for q in range(4):
            acc = rb1[k, 4 * q].astype(F32)
            for h in range(1, 4):
                acc = acc + rb1[k, 4 * q + h].astype(F32)
            for h in range(2):
                tb[k, h, :, q * H : (q + 1) * H] = acc[2 * h : 2 * h + 2].astype(BF)
        v = (k + 4 - r) % 4
        for h in range(2):

            def go(h=h):
                send(tb.at[k, h], rb2.at[y], R2B, r_rb2, dev(p, x, v + 4 * h, c))

            pl.when(v + 4 * h != y)(go)

            @pl.when(v + 4 * h == y)
            def _(h=h):
                rb2[y] = tb[k, h]

    def mixed(e, base, m, back):
        for f in range(2):
            for h in range(2):
                base = base + m[2 * e : 2 * e + 2, 2 * f + h : 2 * f + h + 1] * back[f][h : h + 1, :]
        return base.astype(BF)

    def next_rows():
        arrived(rb2.at[0:7], r_rb2)
        alive = jnp.where(p > 0, 1.0, 0.0).astype(F32)
        m = m_v[...] * alive
        back = []
        for f in range(2):
            acc = rb2[4 * f].astype(F32)
            for h in range(1, 4):
                acc = acc + rb2[4 * f + h].astype(F32)
            back.append(acc)
        for q in range(4):
            for e in range(2):
                rows_b[1, e, :, q * H : (q + 1) * H] = mixed(
                    e,
                    base_v[2 * e : 2 * e + 2, q * Q + H : (q + 1) * Q] * alive,
                    m,
                    [b[:, q * H : (q + 1) * H] for b in back],
                )
        first_b(1)
        arrived(ra2, r_ra2)
        alive = jnp.where(p < 7, 1.0, 0.0).astype(F32)
        m = m_in[...] * alive
        for q in range(4):
            back = []
            for f in range(2):
                acc = ra2[4 * q, f].astype(F32)
                for h in range(1, 4):
                    acc = acc + ra2[4 * q + h, f].astype(F32)
                back.append(acc)
            for e in range(2):
                rows_a[1, q, e] = mixed(e, base_in[q, e] * alive, m, back)
        first_a(1)

    def gather_rows(k):
        pl.when(mine == k)(next_rows)

    hidden_gradient(0)
    hidden_gradient(1)
    input_gradient(0)
    hidden_gradient(2)
    input_gradient(1)
    hidden_gradient(3)
    input_gradient(2)
    to_sources(0)
    input_gradient(3)
    for part in range(2):
        left = jnp.concatenate([avt[part, 0, k] for k in range(K)], axis=1)
        right = (ha, hd)[part][0].reshape(K * 64, H)
        out[0, :, part * H : (part + 1) * H] = dot(left, right, ((1,), (0,)))
    arrived(base_in, r_one.at[2])
    arrived(m_in, r_one.at[3])
    to_sources(1)
    gather_rows(0)
    to_sources(2)
    gather_rows(1)
    to_sources(3)
    second(1, 0)
    gather_rows(2)
    second(1, 1)
    gather_rows(3)
    second(1, 2)
    second(1, 3)
    stores = []
    for k in range(K):
        dispatched(1, k)
        for part in range(2):
            cols = slice(part * H, (part + 1) * H)
            right = ha[1, k].reshape(64, H) if part == 0 else hd[1, k]
            out[0, :, cols] += dot(avt[part, 1, k], right, ((1,), (0,)))

    arrived(ra2.at[0:15], snd.at[D1A])
    arrived(ra2.at[0:15], snd.at[D1A1])
    arrived(rb2.at[0:7], snd.at[D1B])
    arrived(rb2, snd.at[D1B1])
    arrived(ha.at[:, :, 0:7], snd.at[D2A])
    arrived(hb.at[:, :, 0:15], snd.at[D2B])
    arrived(dx.at[:, 0:3], snd.at[DX])
    arrived(ra1.at[:, 0:7], snd.at[R1A])
    arrived(rb1.at[:, 0:15], snd.at[R1B])
    arrived(ra2, snd.at[R2A])
    arrived(rb2.at[0:7], snd.at[R2B])
    arrived(uv.at[0:3], snd.at[UV])
    arrived(sel_in, snd.at[SEL])
    arrived(base_in, snd.at[BASE])
    arrived(m_in, snd.at[MM])
    for cp in stores:
        cp.wait()


def body(cotangent, routes, gates, *others):
    hbm = pl.BlockSpec(memory_space=pl.ANY)
    dma = pltpu.SemaphoreType.DMA
    vmem = pltpu.VMEM
    return pl.pallas_call(
        kernel,
        out_shape=vmem((1, HID, Q), F32),
        in_specs=[hbm] * 8,
        out_specs=pl.BlockSpec(memory_space=vmem),
        scratch_shapes=[
            vmem((TOK, D), BF),
            vmem((2, 8, TOK), jnp.int32),
            vmem((2, 8, TOK), BF),
            vmem((HID, Q), BF),
            vmem((Q, 2 * HID), BF),
            vmem((3, 8, TOK), BF),
            vmem((8, TOK), BF),
            vmem((2, 4, 2, 2, H), BF),
            vmem((2, 2, 2, 4 * H), BF),
            vmem((8, D), F32),
            vmem((4, 2, 2, H), F32),
            vmem((4, 2, 2, H), F32),
            vmem((8, 8), F32),
            vmem((8, 8), F32),
            vmem((4, 2, 2, 32, 2, HID), BF),
            vmem((K, 2, 64, HID), F32),
            vmem((K, 64, 64), BF),
            vmem((2, 2, K, HID, 64), BF),
            vmem((HID, Q), F32),
            vmem((2, K, 4, 2, 2, H), BF),
            vmem((2, K, 2, 8, H), BF),
            vmem((2, 4, 2, 2, 4 * H), BF),
            vmem((2, K, 4, 4, H), BF),
            vmem((2, K, 8, 8, H), BF),
            vmem((2, K, 16, 4, H), BF),
            vmem((2, K, 64, H), BF),
            vmem((K, 4, 64, HID), BF),
            vmem((K, 8, 8, H), BF),
            vmem((K, 16, 4, H), BF),
            vmem((K, 8, 8, H), BF),
            vmem((K, 16, 4, H), BF),
            vmem((K, 4, 2, 2, H), BF),
            vmem((K, 2, 2, 4 * H), BF),
            vmem((16, 2, 2, H), BF),
            vmem((8, 2, 4 * H), BF),
            dma((8,)),
            dma((2,)),
            dma((15,)),
            dma((2, K)),
            dma((2, K)),
            dma((2, K)),
            dma((2, K)),
            dma((K,)),
            dma((K,)),
            dma((K,)),
            dma,
            dma,
            dma((4,)),
        ],
        compiler_params=pltpu.CompilerParams(collective_id=0, has_side_effects=True),
        name="cooldown",
    )(cotangent, jnp.swapaxes(routes, 2, 3), jnp.swapaxes(gates, 2, 3), *others)


def solution(mesh):
    in_specs = (
        P("pipe", ("dp", "expert"), None),
        P("pipe", None, ("dp", "expert"), None),
        P("pipe", None, ("dp", "expert"), None),
        P("pipe", None, "dp", None, None, "expert"),
        P("pipe", None, "dp", None, None, "expert"),
        P("pipe", None, "expert"),
        P("pipe", None, "expert"),
        P("pipe", "expert", None),
    )
    out_specs = P("pipe", "expert", "dp")
    return jax.shard_map(body, mesh=mesh, in_specs=in_specs, out_specs=out_specs, check_vma=False)
```

time: 251 us -> 77.2 us (0.31); the launches traced: 247 us -> 76.8 us
  blocking collectives: 93.6 us -> 0 us
  Pallas kernels: 0 us -> 75.9 us
  waiting for transfers between devices: 55.9 us -> 0 us
  local copies, waits for them, and re-layouts: 50.3 us -> 0.93 us
  other arithmetic: 20.9 us -> 0 us
  starting transfers between devices: 14.9 us -> 0 us
  matrix products: 11.4 us -> 0 us
    all_to_all x3 -> x0, blocking collectives: 93.6 us -> none  [the longest x1 34.3 us: side_by_side(): lax.all_to_all(both, axis, split_axis=split_dim, concat_axis=concat_dim,...]
    pallas_call x0 -> x1, Pallas kernels: none -> 75.9 us  [body(): pl.pallas_call(kernel, out_shape=vmem((1, HID, Q), F32), in_specs=[hbm] *...]
    unnamed x19 -> x1, local copies, waits for them, and re-layouts: 33.2 us -> 0.93 us
    all_to_all x1 -> x0, waiting for transfers between devices: 31 us -> none  [side_by_side(): lax.all_to_all(both, axis, split_axis=split_dim, concat_axis=concat_dim,...]
    ppermute x1 -> x0, waiting for transfers between devices: 24.9 us -> none  [shifted(): return lax.ppermute(block, axis, route)]
    all_to_all x5 -> x0, other arithmetic: 16.5 us -> none  [the longest x4 8.46 us: side_by_side(): lax.all_to_all(both, axis, split_axis=split_dim, concat_axis=concat_dim,...]
    all_to_all x1 -> x0, starting transfers between devices: 13.6 us -> none  [side_by_side(): lax.all_to_all(both, axis, split_axis=split_dim, concat_axis=concat_dim,...]
    dot_general x8 -> x0, matrix products: 11.4 us -> none  [the longest x3 4.68 us: contract_last(): lax.dot_general(left, right, (((1,), (1,)), ((), ())), preferred_element_...]
  transfers between devices with their start and end apart: 2 -> 0, of which waited for: 2 -> 0; matrix products, arithmetic and copies ran while one was open for 0% -> 0% of each run, Pallas kernels for 0% -> 0%
where the time goes in v2:
time: 77.2 us; the launch traced here: 76.8 us
  Pallas kernels  75.9 us (98%)
  local copies, waits for them, and re-layouts  0.93 us (1%)
    pallas_call x1, Pallas kernels, body(): pl.pallas_call(kernel, out_shape=vmem((1, HID, Q), F32), in_specs=[hbm] *...  75.9 us

profile of v2, /device:TPU:1, one launch (start us, length us, event | category | flops | bytes accessed | tf_op | source)
XLA Modules:
  0.0 76.8 jit_solution(13083424416413911095)
XLA Ops:
  0.0 75.9 %cooldown.1 = f32[1,128,1792]{2,1,0:T(8,128)S(1)} custom-call(bf16[1,64,7168]{2,1,0:T(8,128)(2,1)} %cot.1, s32[1,2,8,64]{3,2,1,0:T(8,128)} %bitcast.2, bf16[1,2,8,64]{3,2,1,0:T(8,128)(2,1)} %bitcast.3, bf16[1,2,1,32,2,128]{5,4,3,2,1,0:T(2,128)(2,1)} %gate_pre.1, bf16[1,2,1,32,2,128]{5,4,3,2,1,0:T(2,128)(2,1)} %up_pre.1, bf16[1,7168,128]{2,1,0:T(8,128)(2,1)} %w_gate.1, ...), custom_call_target="tpu_custom_call" | custom-call | tf_op jit(solution)/shard_map/cooldown/pallas_call | solution.py:371
  75.9 0.9 %copy.10 = f32[1,128,1792]{2,1,0:T(8,128)} copy(f32[1,128,1792]{2,1,0:T(8,128)S(1)} %cooldown.1) | data formatting | bytes 1835008

commit v3 on v2

v3 whole, which is shorter than its diff:
```python
import functools

import jax
import jax.numpy as jnp
from jax import lax
from jax.experimental import pallas as pl
from jax.experimental.pallas import tpu as pltpu
from jax.sharding import PartitionSpec as P

MESH = pl.DeviceIdType.MESH
BF = jnp.bfloat16
F32 = jnp.float32

D = 7168
TOK = 64
HID = 128
Q = 1792
HA = 1024
HB = Q - HA
K = 4
FAR = (4, 3, 5, 2, 6, 1, 7)
ROW = tuple((dx, dc) for dx in FAR for dc in (0, 1)) + ((0, 1),)
FORWARD = ((1, 1, 1, 1), (1, 1, 1, 1), (1, 1, 1, 1))
NEAR = tuple((dx, dc) for dx in (2, 6, 1, 7) for dc in (0, 1)) + ((0, 1),)
BACK = ((4, 6, 0, 2), (4, 2, 1, 5), (5, 6, 0, 0), (5, 6, 1, 1), (3, 2, 0, 3), (3, 2, 1, 4))
FAR_ROW = tuple((dx, dc) for dx in (4, 3, 5) for dc in (0, 1))


def dot(a, b, dims):
    return lax.dot_general(a, b, (dims, ((), ())), preferred_element_type=F32)


def kernel(
    cot, routes, gates, gate_pre, up_pre, w_gate, w_up, w_down, out,
    g_v, ids_v, gat_v, w2, w13, sel_s, sel_in, rows_a, rows_b, base_v, base_o, base_in, m_v, m_in, uv, uv1, av1, coef, avt,
    xa, a2, yb, ha, hb, hd, dx, pa, pb, fa, fb, sa, sb, ra1, rb1, ta, tb, ra2, rb2,
    ld, snd, r_xa, r_yb, r_ha, r_hb, r_ha2, r_hb2, r_dx, r_fa, r_fb, r_ra1, r_rb1, r_ra2, r_rb2, r_one,
):
    p = lax.axis_index("pipe")
    r = lax.axis_index("dp")
    s = lax.axis_index("expert")
    y = s // 4
    xh = s % 4
    x = xh * 2 + r // 2
    c = r % 2
    lower = p < 7
    upper = p > 0
    up = jnp.minimum(p + 1, 7)
    down = jnp.maximum(p - 1, 0)
    mine = (r + y) % 4
    half = y // 4
    at = y % 4
    inner = (at == 1) | (at == 2)
    turn = jnp.where(at < 2, 1, -1)

    def dev(p_, x_, y_, c_):
        return (p_, (x_ % 2) * 2 + c_, y_ * 4 + x_ // 2)

    def send(src, dst, kind, recv, target):
        pltpu.make_async_remote_copy(
            src_ref=src, dst_ref=dst, send_sem=snd.at[kind], recv_sem=recv, device_id=target, device_id_type=MESH
        ).start()

    def arrived(like, sem):
        pltpu.make_async_copy(like, like, sem).wait()

    D1A, D1A1, D1B, D1B1, D2A, _, D2F, _, D2B, _, DX, R1A, R1B, R2A, R2B, UV, AV, SEL, BASE, MM = range(20)

    barrier = pltpu.get_barrier_semaphore()
    peers = [((x + ox) % 8, y, (c + oc) % 2, p) for ox, oc in ROW]
    peers += [(x, (y + oy) % 8, c, p) for oy in FAR]
    for x_, y_, c_, p_ in peers:
        pl.semaphore_signal(barrier, inc=1, device_id=dev(p_, x_, y_, c_), device_id_type=MESH)
    for there, p_ in ((lower, up), (upper, down)):
        @pl.when(there)
        def _(p_=p_):
            pl.semaphore_signal(barrier, inc=1, device_id=dev(p_, x, y, c), device_id_type=MESH)

    q0 = pl.multiple_of(r * Q, 128)
    loads = [
        pltpu.make_async_copy(routes.at[0], ids_v, ld.at[0]),
        pltpu.make_async_copy(gates.at[0], gat_v, ld.at[1]),
        pltpu.make_async_copy(cot.at[0], g_v, ld.at[2]),
        pltpu.make_async_copy(w_down.at[0, :, pl.ds(q0, Q)], w2, ld.at[3]),
        pltpu.make_async_copy(w_gate.at[0, pl.ds(q0, Q)], w13.at[:, 0:HID], ld.at[4]),
        pltpu.make_async_copy(w_up.at[0, pl.ds(q0, Q)], w13.at[:, HID : 2 * HID], ld.at[5]),
        pltpu.make_async_copy(gate_pre.at[0, 0, 0], uv.at[r, 0], ld.at[6]),
        pltpu.make_async_copy(up_pre.at[0, 0, 0], uv.at[r, 1], ld.at[7]),
        pltpu.make_async_copy(gate_pre.at[0, 1, 0], uv1.at[0], ld.at[8]),
        pltpu.make_async_copy(up_pre.at[0, 1, 0], uv1.at[1], ld.at[9]),
    ]
    for cp in loads:
        cp.start()

    loads[0].wait()
    loads[1].wait()
    row = lax.broadcasted_iota(jnp.int32, (8, TOK), 0)
    upto = (
        lax.broadcasted_iota(jnp.int32, (TOK, TOK), 0) <= lax.broadcasted_iota(jnp.int32, (TOK, TOK), 1)
    ).astype(F32).astype(BF)
    for t in range(2):
        ids = ids_v[t]
        gat = gat_v[t].astype(F32)
        hit = jnp.zeros((8, TOK), F32)
        gsum = jnp.zeros((8, TOK), F32)
        for e in range(2):
            match = (ids == e).astype(F32)
            of_e = (row >= 2 * e) & (row < 2 * e + 2)
            hit = jnp.where(of_e, jnp.sum(match, axis=0, keepdims=True), hit)
            gsum = jnp.where(of_e, jnp.sum(match * gat, axis=0, keepdims=True), gsum)
        rank = dot(hit.astype(BF), upto, ((1,), (0,))) - 1.0
        sel = hit * (rank == (row & 1).astype(F32)).astype(F32)
        if t == 0:
            sel_s[0] = sel.astype(BF)
        sel_s[1 + t] = (sel * gsum).astype(BF)

    loads[2].wait()
    rows = dot(sel_s[1], g_v[...], ((1,), (0,)))
    for e in range(2):
        for q in range(4):
            rows_a[0, q, e] = rows[2 * e : 2 * e + 2, q * Q : q * Q + HA].astype(BF)
            rows_b[0, e, :, q * HB : (q + 1) * HB] = rows[2 * e : 2 * e + 2, q * Q + HA : (q + 1) * Q].astype(BF)

    for k in range(K):
        if FORWARD[1][k]:
            zeros = jnp.zeros((8, HA), BF)
            ra1[k, (y + 4) % 8] = zeros
            for where, oy in ((1, 3), (2, 5)):
                @pl.when(at != where)
                def _(k=k, oy=oy):
                    ra1[k, (y + oy) % 8] = jnp.zeros((8, HA), BF)

            for where, slot in ((3, 0), (0, 1)):
                @pl.when(at == where)
                def _(k=k, slot=slot):
                    fa[k, slot] = jnp.zeros((8, HA), BF)

            for ox in (3, 4, 5):
                for c_ in range(2):
                    x_ = (x + ox) % 8
                    rb1[k, ((x_ % 2) * 2 + c_) * 4 + x_ // 2] = jnp.zeros((2, 2, HB), BF)

    @pl.when(lower & upper)
    def _():
        pl.semaphore_wait(barrier, len(peers) + 2)

    @pl.when(jnp.logical_not(lower & upper))
    def _():
        pl.semaphore_wait(barrier, len(peers) + 1)

    def first_a(t):
        for ox, oc in ROW:
            x_, c_ = (x + ox) % 8, (c + oc) % 2
            q_ = (x_ % 2) * 2 + c_
            send(rows_a.at[t, q_], xa.at[t, mine, xh], D1A + t, r_xa.at[t, mine], dev(p, x_, y, c_))
        xa[t, mine, xh] = rows_a[t, r]

    def first_b(t):
        for oy in FAR + (0,) * t:
            y_ = (y + oy) % 8
            send(
                rows_b.at[t, y_ // 4], yb.at[t, y % 4, half], D1B + t, r_yb.at[t, mine], dev((p, down)[t], x, y_, c)
            )
        if t == 0:
            yb[t, y % 4, half] = rows_b[t, half]

    def send_b(t, k, x_, c_, sem):
        v = (k + 4 - r) % 4
        columns = pl.ds(pl.multiple_of(((x_ % 2) * 2 + c_) * HB, 128), HB)
        send(yb.at[t, v, :, :, columns], hb.at[t, k, :, v, xh], D2B + t, sem.at[t, k], dev(p, x_, y, c_))

    def second(t, k):
        @pl.when(mine == k)
        def _():
            arrived(xa.at[t, k, 0:3], r_xa.at[t, k])

        @pl.when(mine != k)
        def _():
            arrived(xa.at[t, k], r_xa.at[t, k])

        for e in range(2):
            a2[t, k, e] = jnp.concatenate([xa[t, k, h, e] for h in range(4)], axis=0)
        for oy in (2, 6, 1, 7):
            y_ = (y + oy) % 8
            send(a2.at[t, k, y_ // 4], ha.at[t, k, y], D2A + t, r_ha.at[t, k], dev(p, x, y_, c))

        def direct_a(oy):
            y_ = (y + oy) % 8
            send(a2.at[t, k, y_ // 4], ha.at[t, k, y], D2F + t, r_ha2.at[t, k], dev(p, x, y_, c))

        if FORWARD[2 * t][k]:
            pl.when(at == 1)(functools.partial(direct_a, 3))
            pl.when(at == 2)(functools.partial(direct_a, 5))
        else:
            for oy in (4, 3, 5):
                direct_a(oy)
        ha[t, k, y] = a2[t, k, half]
        v = (k + 4 - r) % 4
        if t == 0:
            @pl.when(mine == k)
            def _():
                arrived(yb.at[t, k, 0], r_yb.at[t, k])

            @pl.when(mine != k)
            def _():
                arrived(yb.at[t, k], r_yb.at[t, k])
        else:
            arrived(yb.at[t, k], r_yb.at[t, k])
        for ox, oc in NEAR:
            send_b(t, k, (x + ox) % 8, (c + oc) % 2, r_hb)
        if not FORWARD[2 * t][k]:
            for ox, oc in FAR_ROW:
                send_b(t, k, (x + ox) % 8, (c + oc) % 2, r_hb2)
        hb[t, k, :, v, xh] = yb[t, v, :, :, pl.ds(pl.multiple_of(r * HB, 128), HB)]

    def landing(k, x_, c_):
        return (k + 4 - ((x_ % 2) * 2 + c_)) % 4, x_ // 2

    def forward(t, k):
        arrived(ha.at[t, k, 0:4], r_ha.at[t, k])

        def pass_a(oy_from, oy_to):
            i = (y + oy_from) % 8
            send(ha.at[t, k, i], ha.at[t, k, i], D2F + t, r_ha2.at[t, k], dev(p, x, (y + oy_to) % 8, c))

        pass_a(8 - 2 * turn, 8 + 2 * turn)
        pl.when(at != 3)(functools.partial(pass_a, 6, 1))
        pl.when(at != 0)(functools.partial(pass_a, 2, 7))
        arrived(nine, r_hb.at[t, k])
        for ox_from, ox_to, cores in ((6, 2, (0,)), (2, 6, (1,)), (7, 2, (0, 1)), (1, 6, (0, 1))):
            for c_ in cores:
                v, i = landing(k, (x + ox_from) % 8, c_)
                send(
                    hb.at[t, k, :, v, i], hb.at[t, k, :, v, i], D2B + t, r_hb2.at[t, k], dev(p, (x + ox_to) % 8, y, c)
                )

    nine, six, fifteen = rb1.at[0, 0:9], rb1.at[0, 0:6], rb1.at[:, 0:15]

    def dispatched(t, k):
        if not FORWARD[2 * t][k]:
            arrived(ha.at[t, k, 0:4], r_ha.at[t, k])
            arrived(nine, r_hb.at[t, k])
        arrived(ha.at[t, k, 0:3], r_ha2.at[t, k])
        arrived(six, r_hb2.at[t, k])
        hd[t, k] = hb[t, k].reshape(64, HB)

    others = [(ol, oc) for ol in (0, 1) for oc in (0, 1) if (ol, oc) != (0, 0)]

    def peer(ol, oc):
        return ((r // 2 + ol) % 2) * 2 + (c + oc) % 2

    first_a(0)
    first_b(0)
    @pl.when(lower)
    def _():
        send(sel_s.at[2], sel_in, SEL, r_one.at[0], dev(up, x, y, c))

    loads[6].wait()
    loads[7].wait()
    for ol, oc in others:
        send(uv.at[r], uv.at[r], UV, r_one.at[1], (p, peer(ol, oc), s))
    loads[8].wait()
    loads[9].wait()
    u, v = (uv1[h].astype(F32).reshape(TOK, HID) for h in range(2))
    av1[r] = (u * jax.nn.sigmoid(u) * v).astype(BF)
    for ol, oc in others:
        send(av1.at[r], av1.at[r], AV, r_one.at[4], (p, peer(ol, oc), s))
    for k in range(K):
        second(0, k)

    for k in range(K):
        if FORWARD[0][k]:
            forward(0, k)

    @pl.when(upper)
    def _():
        arrived(sel_in, r_one.at[0])
        base_v[...] = dot(sel_in[...], g_v[...], ((1,), (0,)))
        m_v[...] = dot(sel_in[...], sel_s[0], ((1,), (1,)))
        for e in range(2):
            for q in range(4):
                base_o[q, e] = base_v[2 * e : 2 * e + 2, q * Q : q * Q + HA]
        send(base_o, base_in, BASE, r_one.at[2], dev(down, x, y, c))
        send(m_v, m_in, MM, r_one.at[3], dev(down, x, y, c))

    arrived(uv.at[0:3], r_one.at[1])
    for k in range(K):
        u, v = (
            jnp.concatenate(
                [uv[(k - yy) % 4, h, 4 * yy : 4 * yy + 4].astype(F32).reshape(8, HID) for yy in range(8)], axis=0
            )
            for h in range(2)
        )
        sig = jax.nn.sigmoid(u)
        act = u * sig
        coef[k, 0] = v * (sig * (1.0 + u * (1.0 - sig)))
        coef[k, 1] = act
        av = (act * v).astype(BF)
        avt[0, k] = av.astype(F32).T.astype(BF)
    loads[3].wait()
    loads[4].wait()
    loads[5].wait()

    def hidden_gradient(k):
        d_a = dot(ha[0, k].reshape(64, HA), w2[:, 0:HA], ((1,), (1,))) + dot(hd[0, k], w2[:, HA:Q], ((1,), (1,)))
        dx[k, r] = d_a.astype(BF)
        for ol, oc in others:
            send(dx.at[k, r], dx.at[k, r], DX, r_dx.at[k], (p, peer(ol, oc), s))

    def input_gradient(k):
        arrived(dx.at[k, 0:3], r_dx.at[k])
        d_act = (dx[k, 0].astype(F32) + dx[k, 1].astype(F32)) + (dx[k, 2].astype(F32) + dx[k, 3].astype(F32))
        d_gu = jnp.concatenate([(d_act * coef[k, 0]).astype(BF), (d_act * coef[k, 1]).astype(BF)], axis=1)
        pa[k] = dot(d_gu, w13[0:HA, :], ((1,), (1,))).astype(BF).reshape(8, 8, HA)

        def far_a(oy_row, oy_to, slot):
            i = (y + oy_row) % 8
            send(pa.at[k, i], fa.at[k, slot], R1A, r_fa.at[k], dev(p, x, (y + oy_to) % 8, c))

        def near_a(oy):
            i = (y + oy) % 8
            send(pa.at[k, i], ra1.at[k, y], R1A, r_ra1.at[k], dev(p, x, i, c))

        if FORWARD[1][k]:
            far_a(4, 8 + 2 * turn, 2)
            pl.when(at != 0)(functools.partial(far_a, 5, 7, 0))
            pl.when(at == 0)(functools.partial(near_a, 5))
            pl.when(at != 3)(functools.partial(far_a, 3, 1, 1))
            pl.when(at == 3)(functools.partial(near_a, 3))
        else:
            for oy in (4, 3, 5, 2, 6):
                near_a(oy)
        near_a(1)
        near_a(7)
        ra1[k, y] = pa[k, y]
        pb[k] = dot(d_gu, w13[HA:Q, :], ((1,), (1,))).astype(BF).reshape(2, 4, 4, 2, HB)

        def near_b(x_, c_):
            v, i = landing(k, x_, c_)
            send(pb.at[k, :, v, i], rb1.at[k, r * 4 + xh], R1B, r_rb1.at[k], dev(p, x_, y, c_))

        if FORWARD[1][k]:
            for ox, ox_to, c_, slot in BACK:
                v, i = landing(k, (x + ox) % 8, c_)
                send(pb.at[k, :, v, i], fb.at[k, slot], R1B, r_fb.at[k], dev(p, (x + ox_to) % 8, y, c))
            for ox, c_ in ((6, 1), (2, 0), (0, 1 - c)):
                near_b((x + ox) % 8, c_)
        else:
            for ox, oc in ROW:
                near_b((x + ox) % 8, (c + oc) % 2)
        v, i = landing(k, x, c)
        rb1[k, r * 4 + xh] = pb[k, :, v, i]

    def forward_back(k):
        @pl.when(inner)
        def _():
            arrived(fa.at[k], r_fa.at[k])

        @pl.when(jnp.logical_not(inner))
        def _():
            arrived(fa.at[k, 0:2], r_fa.at[k])

        tie = fa[k, 2].astype(F32)
        for slot, oy, tied in ((0, 6, at < 2), (1, 2, at >= 2)):
            i = (y + oy) % 8
            acc = pa[k, i].astype(F32) + fa[k, slot].astype(F32) + jnp.where(tied, tie, 0.0)
            sa[k, slot] = acc.astype(BF)
            send(sa.at[k, slot], ra1.at[k, y], R1A, r_ra1.at[k], dev(p, x, i, c))
        arrived(fb.at[k], r_fb.at[k])
        for slot, ox, c_ in ((2, 6, 0), (5, 2, 1), (0, 7, 0), (1, 7, 1), (3, 1, 0), (4, 1, 1)):
            x_ = (x + ox) % 8
            v, i = landing(k, x_, c_)
            acc = pb[k, :, v, i].astype(F32) + fb[k, slot].astype(F32)
            sb[k, slot] = acc.astype(BF)
            send(sb.at[k, slot], rb1.at[k, r * 4 + xh], R1B, r_rb1.at[k], dev(p, x_, y, c_))

    def to_sources(k):
        if FORWARD[1][k]:
            @pl.when(inner)
            def _():
                arrived(ra1.at[k, 0:5], r_ra1.at[k])

            @pl.when(jnp.logical_not(inner))
            def _():
                arrived(ra1.at[k, 0:4], r_ra1.at[k])
        else:
            arrived(ra1.at[k, 0:7], r_ra1.at[k])
        for e in range(2):
            acc = ra1[k, 4 * e].astype(F32)
            for h in range(1, 4):
                acc = acc + ra1[k, 4 * e + h].astype(F32)
            for h in range(4):
                ta[k, h, e] = acc[2 * h : 2 * h + 2].astype(BF)
        r_ = (k + 8 - y) % 4
        for h in range(4):
            send(ta.at[k, h], ra2.at[r * 4 + xh], R2A, r_ra2, (down, r_, y * 4 + h))
        arrived(rb1.at[k, 0 : 9 if FORWARD[1][k] else 15], r_rb1.at[k])
        for q in range(4):
            acc = rb1[k, 4 * q].astype(F32)
            for h in range(1, 4):
                acc = acc + rb1[k, 4 * q + h].astype(F32)
            for h in range(2):
                tb[k, h, :, q * HB : (q + 1) * HB] = acc[h].astype(BF)
        v = (k + 4 - r) % 4
        for h in range(2):

            def go(h=h):
                send(tb.at[k, h], rb2.at[y], R2B, r_rb2, dev(p, x, v + 4 * h, c))

            pl.when(v + 4 * h != y)(go)

            @pl.when(v + 4 * h == y)
            def _(h=h):
                rb2[y] = tb[k, h]

    def mixed(e, base, m, back):
        for f in range(2):
            for h in range(2):
                base = base + m[2 * e : 2 * e + 2, 2 * f + h : 2 * f + h + 1] * back[f][h : h + 1, :]
        return base.astype(BF)

    def next_rows():
        @pl.when(upper)
        def _():
            arrived(rb2.at[0:7], r_rb2)
            back = []
            for f in range(2):
                acc = rb2[4 * f].astype(F32)
                for h in range(1, 4):
                    acc = acc + rb2[4 * f + h].astype(F32)
                back.append(acc)
            for q in range(4):
                for e in range(2):
                    rows_b[1, e, :, q * HB : (q + 1) * HB] = mixed(
                        e,
                        base_v[2 * e : 2 * e + 2, q * Q + HA : (q + 1) * Q],
                        m_v[...],
                        [b[:, q * HB : (q + 1) * HB] for b in back],
                    )
            first_b(1)

        @pl.when(lower)
        def _():
            arrived(ra2, r_ra2)
            for q in range(4):
                back = []
                for f in range(2):
                    acc = ra2[4 * q, f].astype(F32)
                    for h in range(1, 4):
                        acc = acc + ra2[4 * q + h, f].astype(F32)
                    back.append(acc)
                for e in range(2):
                    rows_a[1, q, e] = mixed(e, base_in[q, e], m_in[...], back)
            first_a(1)

    def gather_rows(k):
        pl.when(mine == k)(next_rows)

    for k in range(K):
        dispatched(0, k)
        pl.when(upper)(functools.partial(hidden_gradient, k))
    for k in range(K):
        pl.when(upper)(functools.partial(input_gradient, k))
    left = jnp.concatenate([avt[0, k] for k in range(K)], axis=1)
    out[0, :, 0:HA] = dot(left, ha[0].reshape(K * 64, HA), ((1,), (0,)))
    out[0, :, HA:Q] = dot(left, hd[0].reshape(K * 64, HB), ((1,), (0,)))
    for k in range(K):
        if FORWARD[1][k]:
            pl.when(upper)(functools.partial(forward_back, k))
    arrived(av1.at[0:3], r_one.at[4])
    for k in range(K):
        av = jnp.concatenate([av1[(k - yy) % 4, 8 * yy : 8 * yy + 8] for yy in range(8)], axis=0)
        avt[1, k] = av.astype(F32).T.astype(BF)

    @pl.when(lower)
    def _():
        arrived(base_in, r_one.at[2])
        arrived(m_in, r_one.at[3])

    def if_lower(step, *args):
        pl.when(lower)(functools.partial(step, *args))

    def finish(k):
        dispatched(1, k)
        out[0, :, 0:HA] += dot(avt[1, k], ha[1, k].reshape(64, HA), ((1,), (0,)))
        out[0, :, HA:Q] += dot(avt[1, k], hd[1, k], ((1,), (0,)))

    pl.when(upper)(functools.partial(to_sources, 0))
    pl.when(upper)(functools.partial(to_sources, 1))
    pl.when(upper)(functools.partial(to_sources, 2))
    pl.when(upper)(functools.partial(to_sources, 3))
    gather_rows(0)
    gather_rows(1)
    gather_rows(2)
    gather_rows(3)
    if_lower(second, 1, 0)
    if_lower(second, 1, 1)
    if_lower(second, 1, 2)
    if_lower(second, 1, 3)
    if FORWARD[2][0]:
        if_lower(forward, 1, 0)
    if FORWARD[2][1]:
        if_lower(forward, 1, 1)
    if FORWARD[2][2]:
        if_lower(forward, 1, 2)
    if FORWARD[2][3]:
        if_lower(forward, 1, 3)
    for k in range(K):
        if_lower(finish, k)

    arrived(ra2.at[0:15], snd.at[D1A])
    arrived(rb2.at[0:7], snd.at[D1B])
    arrived(uv.at[0:3], snd.at[UV])
    arrived(av1.at[0:3], snd.at[AV])

    def drain_second(t):
        arrived(ha.at[0, :, 0:4], snd.at[D2A + t])
        direct = FORWARD[2 * t].count(0)
        if direct:
            arrived(ha.at[0, 0:direct, 0:3], snd.at[D2F + t])
        if direct < K:
            @pl.when(inner)
            def _():
                arrived(ha.at[0, direct:K, 0:4], snd.at[D2F + t])

            @pl.when(jnp.logical_not(inner))
            def _():
                arrived(ha.at[0, direct:K, 0:2], snd.at[D2F + t])

        arrived(fifteen, snd.at[D2B + t])

    drain_second(0)

    @pl.when(lower)
    def _():
        drain_second(1)
        arrived(ra2.at[0:15], snd.at[D1A1])
        arrived(sel_in, snd.at[SEL])

    @pl.when(upper)
    def _():
        arrived(rb2, snd.at[D1B1])
        arrived(dx.at[:, 0:3], snd.at[DX])
        arrived(ra1.at[:, 0:7], snd.at[R1A])
        arrived(fifteen, snd.at[R1B])
        arrived(ra2, snd.at[R2A])
        arrived(rb2.at[0:7], snd.at[R2B])
        arrived(base_in, snd.at[BASE])
        arrived(m_in, snd.at[MM])


def body(cotangent, routes, gates, *others):
    hbm = pl.BlockSpec(memory_space=pl.ANY)
    dma = pltpu.SemaphoreType.DMA
    vmem = pltpu.VMEM
    return pl.pallas_call(
        kernel,
        out_shape=vmem((1, HID, Q), F32),
        in_specs=[hbm] * 8,
        out_specs=pl.BlockSpec(memory_space=vmem),
        scratch_shapes=[
            vmem((TOK, D), BF),
            vmem((2, 8, TOK), jnp.int32),
            vmem((2, 8, TOK), BF),
            vmem((HID, Q), BF),
            vmem((Q, 2 * HID), BF),
            vmem((3, 8, TOK), BF),
            vmem((8, TOK), BF),
            vmem((2, 4, 2, 2, HA), BF),
            vmem((2, 2, 2, 4 * HB), BF),
            vmem((8, D), F32),
            vmem((4, 2, 2, HA), F32),
            vmem((4, 2, 2, HA), F32),
            vmem((8, 8), F32),
            vmem((8, 8), F32),
            vmem((4, 2, 32, 2, HID), BF),
            vmem((2, 32, 2, HID), BF),
            vmem((4, TOK, HID), BF),
            vmem((K, 2, 64, HID), F32),
            vmem((2, K, HID, 64), BF),
            vmem((2, K, 4, 2, 2, HA), BF),
            vmem((2, K, 2, 8, HA), BF),
            vmem((2, 4, 2, 2, 4 * HB), BF),
            vmem((2, K, 8, 8, HA), BF),
            vmem((2, K, 2, 4, 4, 2, HB), BF),
            vmem((2, K, 64, HB), BF),
            vmem((K, 4, 64, HID), BF),
            vmem((K, 8, 8, HA), BF),
            vmem((K, 2, 4, 4, 2, HB), BF),
            vmem((K, 3, 8, HA), BF),
            vmem((K, 6, 2, 2, HB), BF),
            vmem((K, 2, 8, HA), BF),
            vmem((K, 6, 2, 2, HB), BF),
            vmem((K, 8, 8, HA), BF),
            vmem((K, 16, 2, 2, HB), BF),
            vmem((K, 4, 2, 2, HA), BF),
            vmem((K, 2, 2, 4 * HB), BF),
            vmem((16, 2, 2, HA), BF),
            vmem((8, 2, 4 * HB), BF),
            dma((10,)),
            dma((20,)),
            dma((2, K)),
            dma((2, K)),
            dma((2, K)),
            dma((2, K)),
            dma((2, K)),
            dma((2, K)),
            dma((K,)),
            dma((K,)),
            dma((K,)),
            dma((K,)),
            dma((K,)),
            dma,
            dma,
            dma((5,)),
        ],
        compiler_params=pltpu.CompilerParams(collective_id=0, has_side_effects=True),
        name="cooldown",
    )(cotangent, jnp.swapaxes(routes, 2, 3), jnp.swapaxes(gates, 2, 3), *others)


def solution(mesh):
    in_specs = (
        P("pipe", ("dp", "expert"), None),
        P("pipe", None, ("dp", "expert"), None),
        P("pipe", None, ("dp", "expert"), None),
        P("pipe", None, "dp", None, None, "expert"),
        P("pipe", None, "dp", None, None, "expert"),
        P("pipe", None, "expert"),
        P("pipe", None, "expert"),
        P("pipe", "expert", None),
    )
    out_specs = P("pipe", "expert", "dp")
    return jax.shard_map(body, mesh=mesh, in_specs=in_specs, out_specs=out_specs, check_vma=False)
```

time: 77.2 us -> 66.7 us (0.86)
  Pallas kernels: 75.9 us -> 65.3 us
    pallas_call x1, Pallas kernels: 75.9 us -> 65.3 us  [body(): pl.pallas_call(kernel, out_shape=vmem((1, HID, Q), F32), in_specs=[hbm] *...]
where the time goes in v3:
time: 66.7 us; the launch traced here: 66.2 us
  Pallas kernels  65.3 us (98%)
  local copies, waits for them, and re-layouts  0.93 us (1%)
    pallas_call x1, Pallas kernels, body(): pl.pallas_call(kernel, out_shape=vmem((1, HID, Q), F32), in_specs=[hbm] *...  65.3 us

profile of v3, /device:TPU:1, one launch (start us, length us, event | category | flops | bytes accessed | tf_op | source)
XLA Modules:
  0.0 66.2 jit_solution(9302675806032393507)
XLA Ops:
  0.0 65.3 %cooldown.1 = f32[1,128,1792]{2,1,0:T(8,128)S(1)} custom-call(bf16[1,64,7168]{2,1,0:T(8,128)(2,1)} %cot.1, s32[1,2,8,64]{3,2,1,0:T(8,128)} %bitcast.2, bf16[1,2,8,64]{3,2,1,0:T(8,128)(2,1)} %bitcast.3, bf16[1,2,1,32,2,128]{5,4,3,2,1,0:T(2,128)(2,1)} %gate_pre.1, bf16[1,2,1,32,2,128]{5,4,3,2,1,0:T(2,128)(2,1)} %up_pre.1, bf16[1,7168,128]{2,1,0:T(8,128)(2,1)} %w_gate.1, ...), custom_call_target="tpu_custom_call" | custom-call | tf_op jit(solution)/shard_map/cooldown/pallas_call | solution.py:556
  65.3 0.9 %copy.10 = f32[1,128,1792]{2,1,0:T(8,128)} copy(f32[1,128,1792]{2,1,0:T(8,128)S(1)} %cooldown.1) | data formatting | bytes 1835008

commit v4 on v3

--- a/solution.py
+++ b/solution.py
@@ -15,7 +15,7 @@
 TOK = 64
 HID = 128
 Q = 1792
-HA = 1024
+HA = 896
 HB = Q - HA
 K = 4
 FAR = (4, 3, 5, 2, 6, 1, 7)
@@ -34,7 +34,7 @@
     cot, routes, gates, gate_pre, up_pre, w_gate, w_up, w_down, out,
     g_v, ids_v, gat_v, w2, w13, sel_s, sel_in, rows_a, rows_b, base_v, base_o, base_in, m_v, m_in, uv, uv1, av1, coef, avt,
     xa, a2, yb, ha, hb, hd, dx, pa, pb, fa, fb, sa, sb, ra1, rb1, ta, tb, ra2, rb2,
-    ld, snd, r_xa, r_yb, r_ha, r_hb, r_ha2, r_hb2, r_dx, r_fa, r_fb, r_ra1, r_rb1, r_ra2, r_rb2, r_one,
+    ld, snd, r_xa, r_yb, r_ha, r_hb, r_ha2, r_hb2, r_dx, r_fa, r_fb, r_ra1, r_rb1, r_ra2, r_rb2, r_one, ready,
 ):
     p = lax.axis_index("pipe")
     r = lax.axis_index("dp")
@@ -71,10 +71,14 @@
     peers += [(x, (y + oy) % 8, c, p) for oy in FAR]
     for x_, y_, c_, p_ in peers:
         pl.semaphore_signal(barrier, inc=1, device_id=dev(p_, x_, y_, c_), device_id_type=MESH)
-    for there, p_ in ((lower, up), (upper, down)):
-        @pl.when(there)
-        def _(p_=p_):
-            pl.semaphore_signal(barrier, inc=1, device_id=dev(p_, x, y, c), device_id_type=MESH)
+
+    @pl.when(lower & upper)
+    def _():
+        pl.semaphore_signal(barrier, inc=1, device_id=dev(up, x, y, c), device_id_type=MESH)
+
+    @pl.when(p == 1)
+    def _():
+        pl.semaphore_signal(barrier, inc=1, device_id=dev(down, x, y, c), device_id_type=MESH)
 
     q0 = pl.multiple_of(r * Q, 128)
     loads = [
@@ -140,13 +144,17 @@
                     x_ = (x + ox) % 8
                     rb1[k, ((x_ % 2) * 2 + c_) * 4 + x_ // 2] = jnp.zeros((2, 2, HB), BF)
 
-    @pl.when(lower & upper)
-    def _():
-        pl.semaphore_wait(barrier, len(peers) + 2)
-
-    @pl.when(jnp.logical_not(lower & upper))
+    @pl.when(p != 1)
     def _():
         pl.semaphore_wait(barrier, len(peers) + 1)
+
+    @pl.when(p == 1)
+    def _():
+        pl.semaphore_wait(barrier, len(peers))
+
+    @pl.when(p > 1)
+    def _():
+        pl.semaphore_signal(ready, inc=1, device_id=dev(down, x, y, c), device_id_type=MESH)
 
     def first_a(t):
         for ox, oc in ROW:
@@ -169,6 +177,10 @@
         columns = pl.ds(pl.multiple_of(((x_ % 2) * 2 + c_) * HB, 128), HB)
         send(yb.at[t, v, :, :, columns], hb.at[t, k, :, v, xh], D2B + t, sem.at[t, k], dev(p, x_, y, c_))
 
+    def direct_a(t, k, oy):
+        y_ = (y + oy) % 8
+        send(a2.at[t, k, y_ // 4], ha.at[t, k, y], D2F + t, r_ha2.at[t, k], dev(p, x, y_, c))
+
     def second(t, k):
         @pl.when(mine == k)
         def _():
@@ -183,17 +195,9 @@
         for oy in (2, 6, 1, 7):
             y_ = (y + oy) % 8
             send(a2.at[t, k, y_ // 4], ha.at[t, k, y], D2A + t, r_ha.at[t, k], dev(p, x, y_, c))
-
-        def direct_a(oy):
-            y_ = (y + oy) % 8
-            send(a2.at[t, k, y_ // 4], ha.at[t, k, y], D2F + t, r_ha2.at[t, k], dev(p, x, y_, c))
-
-        if FORWARD[2 * t][k]:
-            pl.when(at == 1)(functools.partial(direct_a, 3))
-            pl.when(at == 2)(functools.partial(direct_a, 5))
-        else:
+        if not FORWARD[2 * t][k]:
             for oy in (4, 3, 5):
-                direct_a(oy)
+                direct_a(t, k, oy)
         ha[t, k, y] = a2[t, k, half]
         v = (k + 4 - r) % 4
         if t == 0:
@@ -217,6 +221,8 @@
         return (k + 4 - ((x_ % 2) * 2 + c_)) % 4, x_ // 2
 
     def forward(t, k):
+        pl.when(at == 1)(functools.partial(direct_a, t, k, 3))
+        pl.when(at == 2)(functools.partial(direct_a, t, k, 5))
         arrived(ha.at[t, k, 0:4], r_ha.at[t, k])
 
         def pass_a(oy_from, oy_to):
@@ -251,10 +257,6 @@
 
     first_a(0)
     first_b(0)
-    @pl.when(lower)
-    def _():
-        send(sel_s.at[2], sel_in, SEL, r_one.at[0], dev(up, x, y, c))
-
     loads[6].wait()
     loads[7].wait()
     for ol, oc in others:
@@ -265,6 +267,14 @@
     av1[r] = (u * jax.nn.sigmoid(u) * v).astype(BF)
     for ol, oc in others:
         send(av1.at[r], av1.at[r], AV, r_one.at[4], (p, peer(ol, oc), s))
+    @pl.when(lower & upper)
+    def _():
+        pl.semaphore_wait(ready, 1)
+
+    @pl.when(lower)
+    def _():
+        send(sel_s.at[2], sel_in, SEL, r_one.at[0], dev(up, x, y, c))
+
     for k in range(K):
         second(0, k)
 
@@ -307,6 +317,14 @@
         for ol, oc in others:
             send(dx.at[k, r], dx.at[k, r], DX, r_dx.at[k], (p, peer(ol, oc), s))
 
+    def near_a(k, oy):
+        i = (y + oy) % 8
+        send(pa.at[k, i], ra1.at[k, y], R1A, r_ra1.at[k], dev(p, x, i, c))
+
+    def near_b(k, x_, c_):
+        v, i = landing(k, x_, c_)
+        send(pb.at[k, :, v, i], rb1.at[k, r * 4 + xh], R1B, r_rb1.at[k], dev(p, x_, y, c_))
+
     def input_gradient(k):
         arrived(dx.at[k, 0:3], r_dx.at[k])
         d_act = (dx[k, 0].astype(F32) + dx[k, 1].astype(F32)) + (dx[k, 2].astype(F32) + dx[k, 3].astype(F32))
@@ -317,41 +335,35 @@
             i = (y + oy_row) % 8
             send(pa.at[k, i], fa.at[k, slot], R1A, r_fa.at[k], dev(p, x, (y + oy_to) % 8, c))
 
-        def near_a(oy):
-            i = (y + oy) % 8
-            send(pa.at[k, i], ra1.at[k, y], R1A, r_ra1.at[k], dev(p, x, i, c))
-
         if FORWARD[1][k]:
             far_a(4, 8 + 2 * turn, 2)
             pl.when(at != 0)(functools.partial(far_a, 5, 7, 0))
-            pl.when(at == 0)(functools.partial(near_a, 5))
+            pl.when(at == 0)(functools.partial(near_a, k, 5))
             pl.when(at != 3)(functools.partial(far_a, 3, 1, 1))
-            pl.when(at == 3)(functools.partial(near_a, 3))
+            pl.when(at == 3)(functools.partial(near_a, k, 3))
         else:
             for oy in (4, 3, 5, 2, 6):
-                near_a(oy)
-        near_a(1)
-        near_a(7)
+                near_a(k, oy)
+            near_a(k, 1)
+            near_a(k, 7)
         ra1[k, y] = pa[k, y]
         pb[k] = dot(d_gu, w13[HA:Q, :], ((1,), (1,))).astype(BF).reshape(2, 4, 4, 2, HB)
-
-        def near_b(x_, c_):
-            v, i = landing(k, x_, c_)
-            send(pb.at[k, :, v, i], rb1.at[k, r * 4 + xh], R1B, r_rb1.at[k], dev(p, x_, y, c_))
 
         if FORWARD[1][k]:
             for ox, ox_to, c_, slot in BACK:
                 v, i = landing(k, (x + ox) % 8, c_)
                 send(pb.at[k, :, v, i], fb.at[k, slot], R1B, r_fb.at[k], dev(p, (x + ox_to) % 8, y, c))
-            for ox, c_ in ((6, 1), (2, 0), (0, 1 - c)):
-                near_b((x + ox) % 8, c_)
         else:
             for ox, oc in ROW:
-                near_b((x + ox) % 8, (c + oc) % 2)
+                near_b(k, (x + ox) % 8, (c + oc) % 2)
         v, i = landing(k, x, c)
         rb1[k, r * 4 + xh] = pb[k, :, v, i]
 
     def forward_back(k):
+        near_a(k, 1)
+        near_a(k, 7)
+        for ox, c_ in ((6, 1), (2, 0), (0, 1 - c)):
+            near_b(k, (x + ox) % 8, c_)
         @pl.when(inner)
         def _():
             arrived(fa.at[k], r_fa.at[k])
@@ -613,6 +625,7 @@
             dma,
             dma,
             dma((5,)),
+            pltpu.SemaphoreType.REGULAR,
         ],
         compiler_params=pltpu.CompilerParams(collective_id=0, has_side_effects=True),
         name="cooldown",

time: 66.7 us -> 62.6 us (0.939)
  the two profiles are of different devices: /device:TPU:1 before, /device:TPU:384 now
where the time goes in v4:
time: 62.6 us; the launch traced here: 62.4 us
  Pallas kernels  61.5 us (98%)
  local copies, waits for them, and re-layouts  0.93 us (1%)
    pallas_call x1, Pallas kernels, body(): pl.pallas_call(kernel, out_shape=vmem((1, HID, Q), F32), in_specs=[hbm] *...  61.5 us

profile of v4, /device:TPU:384, one launch (start us, length us, event | category | flops | bytes accessed | tf_op | source)
XLA Modules:
  0.0 62.4 jit_solution(4077040823622474164)
XLA Ops:
  0.0 61.5 %cooldown.1 = f32[1,128,1792]{2,1,0:T(8,128)S(1)} custom-call(bf16[1,64,7168]{2,1,0:T(8,128)(2,1)} %cot.1, s32[1,2,8,64]{3,2,1,0:T(8,128)} %bitcast.2, bf16[1,2,8,64]{3,2,1,0:T(8,128)(2,1)} %bitcast.3, bf16[1,2,1,32,2,128]{5,4,3,2,1,0:T(2,128)(2,1)} %gate_pre.1, bf16[1,2,1,32,2,128]{5,4,3,2,1,0:T(2,128)(2,1)} %up_pre.1, bf16[1,7168,128]{2,1,0:T(8,128)(2,1)} %w_gate.1, ...), custom_call_target="tpu_custom_call" | custom-call | tf_op jit(solution)/shard_map/cooldown/pallas_call | solution.py:568
  61.5 0.9 %copy.10 = f32[1,128,1792]{2,1,0:T(8,128)} copy(f32[1,128,1792]{2,1,0:T(8,128)S(1)} %cooldown.1) | data formatting | bytes 1835008

commit v5 on v4

v5 whole, which is shorter than its diff:
```python
import functools

import jax
import jax.numpy as jnp
from jax import lax
from jax.experimental import pallas as pl
from jax.experimental.pallas import tpu as pltpu
from jax.sharding import PartitionSpec as P

MESH = pl.DeviceIdType.MESH
BF = jnp.bfloat16
F32 = jnp.float32

D = 7168
TOK = 64
HID = 128
Q = 1792
HA = HB = 896
K = 4
FAR = (4, 3, 5, 2, 6, 1, 7)
ROW = tuple((dx, dc) for dx in FAR for dc in (0, 1)) + ((0, 1),)
NEAR = tuple((dx, dc) for dx in (2, 6, 1, 7) for dc in (0, 1)) + ((0, 1),)
BACK = ((4, 6, 0, 2), (4, 2, 1, 5), (5, 6, 0, 0), (5, 6, 1, 1), (3, 2, 0, 3), (3, 2, 1, 4))
A8, B4, ROWS2, DX64, UV128 = 14, 7, 14, 16, 32


def dot(a, b, dims):
    return lax.dot_general(a, b, (dims, ((), ())), preferred_element_type=F32)


def kernel(
    cot, routes, gates, gate_pre, up_pre, w_gate, w_up, w_down, out,
    g_v, ids_v, gat_v, w2, w13, w2t, w13t, sel_s, sel_in, rows_a, rows_b, base_v, base_o, base_in, m_v, m_in, uv, uv1, av1, coef, avt,
    void, xa, a2, yb, ha, hb, hd, dx, pa, pb, fa, fb, sa, sb, ra1, rb1, ta, tb, ra2, rb2,
    ld, snd, r_x, r_near, r_far, r_dx, r_f, r_back, r_ra2, r_rb2, r_one, ready, r_x2, r_near2, r_f2, r_back2,
):
    p = lax.axis_index("pipe")
    r = lax.axis_index("dp")
    s = lax.axis_index("expert")
    y = s // 4
    xh = s % 4
    x = xh * 2 + r // 2
    c = r % 2
    lower = p < 7
    upper = p > 0
    up = jnp.minimum(p + 1, 7)
    down = jnp.maximum(p - 1, 0)
    mine = (r + y) % 4
    half = y // 4
    at = y % 4
    inner = (at == 1) | (at == 2)
    turn = jnp.where(at < 2, 1, -1)

    def dev(p_, x_, y_, c_):
        return (p_, (x_ % 2) * 2 + c_, y_ * 4 + x_ // 2)

    def send(src, dst, kind, recv, target):
        pltpu.make_async_remote_copy(
            src_ref=src, dst_ref=dst, send_sem=snd.at[kind], recv_sem=recv, device_id=target, device_id_type=MESH
        ).start()

    def arrived(like, sem):
        pltpu.make_async_copy(like, like, sem).wait()

    def arrived_kib(size, sem):
        arrived(void.at[0:size], sem)

    ALL, LOWER, UPPER, SEL, MM = range(5)

    barrier = pltpu.get_barrier_semaphore()
    peers = [((x + ox) % 8, y, (c + oc) % 2, p) for ox, oc in ROW]
    peers += [(x, (y + oy) % 8, c, p) for oy in FAR]
    for x_, y_, c_, p_ in peers:
        pl.semaphore_signal(barrier, inc=1, device_id=dev(p_, x_, y_, c_), device_id_type=MESH)

    @pl.when(lower & upper)
    def _():
        pl.semaphore_signal(barrier, inc=1, device_id=dev(up, x, y, c), device_id_type=MESH)

    @pl.when(p == 1)
    def _():
        pl.semaphore_signal(barrier, inc=1, device_id=dev(down, x, y, c), device_id_type=MESH)

    q0 = pl.multiple_of(r * Q, 128)
    loads = [
        pltpu.make_async_copy(routes.at[0], ids_v, ld.at[0]),
        pltpu.make_async_copy(gates.at[0], gat_v, ld.at[1]),
        pltpu.make_async_copy(cot.at[0], g_v, ld.at[2]),
        pltpu.make_async_copy(w_down.at[0, :, pl.ds(q0, Q)], w2, ld.at[3]),
        pltpu.make_async_copy(w_gate.at[0, pl.ds(q0, Q)], w13.at[:, 0:HID], ld.at[3]),
        pltpu.make_async_copy(w_up.at[0, pl.ds(q0, Q)], w13.at[:, HID : 2 * HID], ld.at[3]),
        pltpu.make_async_copy(gate_pre.at[0, 0, 0], uv.at[r, 0], ld.at[4]),
        pltpu.make_async_copy(up_pre.at[0, 0, 0], uv.at[r, 1], ld.at[4]),
        pltpu.make_async_copy(gate_pre.at[0, 1, 0], uv1.at[0], ld.at[4]),
        pltpu.make_async_copy(up_pre.at[0, 1, 0], uv1.at[1], ld.at[4]),
    ]
    for cp in loads:
        cp.start()

    loads[0].wait()
    loads[1].wait()
    row = lax.broadcasted_iota(jnp.int32, (8, TOK), 0)
    upto = (
        lax.broadcasted_iota(jnp.int32, (TOK, TOK), 0) <= lax.broadcasted_iota(jnp.int32, (TOK, TOK), 1)
    ).astype(F32).astype(BF)
    for t in range(2):
        ids = ids_v[t]
        gat = gat_v[t].astype(F32)
        hit = jnp.zeros((8, TOK), F32)
        gsum = jnp.zeros((8, TOK), F32)
        for e in range(2):
            match = (ids == e).astype(F32)
            of_e = (row >= 2 * e) & (row < 2 * e + 2)
            hit = jnp.where(of_e, jnp.sum(match, axis=0, keepdims=True), hit)
            gsum = jnp.where(of_e, jnp.sum(match * gat, axis=0, keepdims=True), gsum)
        rank = dot(hit.astype(BF), upto, ((1,), (0,))) - 1.0
        sel = hit * (rank == (row & 1).astype(F32)).astype(F32)
        if t == 0:
            sel_s[0] = sel.astype(BF)
        sel_s[1 + t] = (sel * gsum).astype(BF)

    loads[2].wait()
    rows = dot(sel_s[1], g_v[...], ((1,), (0,)))
    for e in range(2):
        for q in range(4):
            rows_a[0, q, e] = rows[2 * e : 2 * e + 2, q * Q : q * Q + HA].astype(BF)
            rows_b[0, e, :, q * HB : (q + 1) * HB] = rows[2 * e : 2 * e + 2, q * Q + HA : (q + 1) * Q].astype(BF)

    for k in range(K):
        ra1[k, (y + 4) % 8] = jnp.zeros((8, HA), BF)
        for where, oy in ((1, 3), (2, 5)):
            @pl.when(at != where)
            def _(k=k, oy=oy):
                ra1[k, (y + oy) % 8] = jnp.zeros((8, HA), BF)

        for where, slot in ((3, 0), (0, 1)):
            @pl.when(at == where)
            def _(k=k, slot=slot):
                fa[k, slot] = jnp.zeros((8, HA), BF)

        for ox in (3, 4, 5):
            for c_ in range(2):
                x_ = (x + ox) % 8
                rb1[k, ((x_ % 2) * 2 + c_) * 4 + x_ // 2] = jnp.zeros((2, 2, HB), BF)

    @pl.when(p != 1)
    def _():
        pl.semaphore_wait(barrier, len(peers) + 1)

    @pl.when(p == 1)
    def _():
        pl.semaphore_wait(barrier, len(peers))

    @pl.when(p > 1)
    def _():
        pl.semaphore_signal(ready, inc=1, device_id=dev(down, x, y, c), device_id_type=MESH)

    def first_a(t):
        for ox, oc in ROW:
            x_, c_ = (x + ox) % 8, (c + oc) % 2
            q_ = (x_ % 2) * 2 + c_
            send(rows_a.at[t, q_], xa.at[t, mine, xh], (ALL, LOWER)[t], r_x.at[t, mine], dev(p, x_, y, c_))
        xa[t, mine, xh] = rows_a[t, r]

    def first_b(t):
        for oy in FAR + (0,) * t:
            y_ = (y + oy) % 8
            send(
                rows_b.at[t, y_ // 4], yb.at[t, y % 4, half], (ALL, UPPER)[t], r_x2.at[t, mine], dev((p, down)[t], x, y_, c)
            )
        if t == 0:
            yb[t, y % 4, half] = rows_b[t, half]

    def send_b(t, k, x_, c_):
        v = (k + 4 - r) % 4
        columns = pl.ds(pl.multiple_of(((x_ % 2) * 2 + c_) * HB, 128), HB)
        send(yb.at[t, v, :, :, columns], hb.at[t, k, :, v, xh], (ALL, LOWER)[t], r_near2.at[t, k], dev(p, x_, y, c_))

    def direct_a(t, k, oy):
        y_ = (y + oy) % 8
        send(a2.at[t, k, y_ // 4], ha.at[t, k, y], (ALL, LOWER)[t], r_far.at[t, k], dev(p, x, y_, c))

    def second(t, k):
        @pl.when(mine == k)
        def _():
            arrived_kib(3 * B4, r_x.at[t, k])

        @pl.when(mine != k)
        def _():
            arrived_kib(4 * B4, r_x.at[t, k])

        for e in range(2):
            a2[t, k, e] = jnp.concatenate([xa[t, k, h, e] for h in range(4)], axis=0)
        for oy in (2, 6, 1, 7):
            y_ = (y + oy) % 8
            send(a2.at[t, k, y_ // 4], ha.at[t, k, y], (ALL, LOWER)[t], r_near.at[t, k], dev(p, x, y_, c))
        ha[t, k, y] = a2[t, k, half]
        if t == 0:
            @pl.when(mine == k)
            def _():
                arrived_kib(ROWS2, r_x2.at[t, k])

            @pl.when(mine != k)
            def _():
                arrived_kib(2 * ROWS2, r_x2.at[t, k])
        else:
            arrived_kib(2 * ROWS2, r_x2.at[t, k])
        v = (k + 4 - r) % 4
        for ox, oc in NEAR:
            send_b(t, k, (x + ox) % 8, (c + oc) % 2)
        hb[t, k, :, v, xh] = yb[t, v, :, :, pl.ds(pl.multiple_of(r * HB, 128), HB)]

    def landing(k, x_, c_):
        return (k + 4 - ((x_ % 2) * 2 + c_)) % 4, x_ // 2

    def forward(t, k):
        pl.when(at == 1)(functools.partial(direct_a, t, k, 3))
        pl.when(at == 2)(functools.partial(direct_a, t, k, 5))
        arrived_kib(4 * A8, r_near.at[t, k])

        def pass_a(oy_from, oy_to):
            i = (y + oy_from) % 8
            send(ha.at[t, k, i], ha.at[t, k, i], (ALL, LOWER)[t], r_far.at[t, k], dev(p, x, (y + oy_to) % 8, c))

        pass_a(8 - 2 * turn, 8 + 2 * turn)
        pl.when(at != 3)(functools.partial(pass_a, 6, 1))
        pl.when(at != 0)(functools.partial(pass_a, 2, 7))
        arrived_kib(9 * B4, r_near2.at[t, k])
        for ox_from, ox_to, cores in ((6, 2, (0,)), (2, 6, (1,)), (7, 2, (0, 1)), (1, 6, (0, 1))):
            for c_ in cores:
                v, i = landing(k, (x + ox_from) % 8, c_)
                send(
                    hb.at[t, k, :, v, i], hb.at[t, k, :, v, i], (ALL, LOWER)[t], r_far.at[t, k], dev(p, (x + ox_to) % 8, y, c)
                )

    def dispatched(t, k):
        arrived_kib(3 * A8 + 6 * B4, r_far.at[t, k])
        hd[t, k] = hb[t, k].reshape(64, HB)

    others = [(ol, oc) for ol in (0, 1) for oc in (0, 1) if (ol, oc) != (0, 0)]

    def peer(ol, oc):
        return ((r // 2 + ol) % 2) * 2 + (c + oc) % 2

    first_a(0)
    first_b(0)
    arrived_kib(2 * UV128, ld.at[4])
    for ol, oc in others:
        send(uv.at[r], uv.at[r], ALL, r_one.at[1], (p, peer(ol, oc), s))
    u, v = (uv1[h].astype(F32).reshape(TOK, HID) for h in range(2))
    av1[r] = (u * jax.nn.sigmoid(u) * v).astype(BF)
    for ol, oc in others:
        send(av1.at[r], av1.at[r], ALL, r_one.at[4], (p, peer(ol, oc), s))
    @pl.when(lower & upper)
    def _():
        pl.semaphore_wait(ready, 1)

    @pl.when(lower)
    def _():
        send(sel_s.at[2], sel_in, SEL, r_one.at[0], dev(up, x, y, c))

    for k in range(K):
        second(0, k)

    arrived_kib(3 * Q // 4, ld.at[3])
    w2t[...] = w2[...].astype(F32).T.astype(BF)
    w13t[...] = w13[...].astype(F32).T.astype(BF)
    for k in range(K):
        forward(0, k)

    @pl.when(upper)
    def _():
        arrived(sel_in, r_one.at[0])
        base_v[...] = dot(sel_in[...], g_v[...], ((1,), (0,)))
        m_v[...] = dot(sel_in[...], sel_s[0], ((1,), (1,)))
        for e in range(2):
            for q in range(4):
                base_o[q, e] = base_v[2 * e : 2 * e + 2, q * Q : q * Q + HA]
        send(base_o, base_in, UPPER, r_one.at[2], dev(down, x, y, c))
        send(m_v, m_in, MM, r_one.at[3], dev(down, x, y, c))

    arrived(uv.at[0:3], r_one.at[1])
    for k in range(K):
        u, v = (
            jnp.concatenate(
                [uv[(k - yy) % 4, h, 4 * yy : 4 * yy + 4].astype(F32).reshape(8, HID) for yy in range(8)], axis=0
            )
            for h in range(2)
        )
        sig = jax.nn.sigmoid(u)
        act = u * sig
        coef[k, 0] = v * (sig * (1.0 + u * (1.0 - sig)))
        coef[k, 1] = act
        av = (act * v).astype(BF)
        avt[0, k] = av.astype(F32).T.astype(BF)

    def hidden_gradient(k):
        d_a = dot(ha[0, k].reshape(64, HA), w2t[0:HA], ((1,), (0,))) + dot(hd[0, k], w2t[HA:Q], ((1,), (0,)))
        dx[k, r] = d_a.astype(BF)
        for ol, oc in others:
            send(dx.at[k, r], dx.at[k, r], UPPER, r_dx.at[k], (p, peer(ol, oc), s))

    def near_a(k, oy):
        i = (y + oy) % 8
        send(pa.at[k, i], ra1.at[k, y], UPPER, r_back.at[k], dev(p, x, i, c))

    def near_b(k, x_, c_):
        v, i = landing(k, x_, c_)
        send(pb.at[k, :, v, i], rb1.at[k, r * 4 + xh], UPPER, r_back2.at[k], dev(p, x_, y, c_))

    def input_gradient(k):
        arrived(dx.at[k, 0:3], r_dx.at[k])
        d_act = (dx[k, 0].astype(F32) + dx[k, 1].astype(F32)) + (dx[k, 2].astype(F32) + dx[k, 3].astype(F32))
        d_gu = jnp.concatenate([(d_act * coef[k, 0]).astype(BF), (d_act * coef[k, 1]).astype(BF)], axis=1)
        pa[k] = dot(d_gu, w13t[:, 0:HA], ((1,), (0,))).astype(BF).reshape(8, 8, HA)

        def far_a(oy_row, oy_to, slot):
            i = (y + oy_row) % 8
            send(pa.at[k, i], fa.at[k, slot], UPPER, r_f.at[k], dev(p, x, (y + oy_to) % 8, c))

        far_a(4, 8 + 2 * turn, 2)
        pl.when(at != 0)(functools.partial(far_a, 5, 7, 0))
        pl.when(at == 0)(functools.partial(near_a, k, 5))
        pl.when(at != 3)(functools.partial(far_a, 3, 1, 1))
        pl.when(at == 3)(functools.partial(near_a, k, 3))
        ra1[k, y] = pa[k, y]
        pb[k] = dot(d_gu, w13t[:, HA:Q], ((1,), (0,))).astype(BF).reshape(2, 4, 4, 2, HB)

        for ox, ox_to, c_, slot in BACK:
            v, i = landing(k, (x + ox) % 8, c_)
            send(pb.at[k, :, v, i], fb.at[k, slot], UPPER, r_f2.at[k], dev(p, (x + ox_to) % 8, y, c))
        v, i = landing(k, x, c)
        rb1[k, r * 4 + xh] = pb[k, :, v, i]

    def forward_back(k):
        near_a(k, 1)
        near_a(k, 7)
        for ox, c_ in ((6, 1), (2, 0), (0, 1 - c)):
            near_b(k, (x + ox) % 8, c_)
        @pl.when(inner)
        def _():
            arrived_kib(3 * A8, r_f.at[k])

        @pl.when(jnp.logical_not(inner))
        def _():
            arrived_kib(2 * A8, r_f.at[k])

        tie = fa[k, 2].astype(F32)
        for slot, oy, tied in ((0, 6, at < 2), (1, 2, at >= 2)):
            i = (y + oy) % 8
            acc = pa[k, i].astype(F32) + fa[k, slot].astype(F32) + jnp.where(tied, tie, 0.0)
            sa[k, slot] = acc.astype(BF)
            send(sa.at[k, slot], ra1.at[k, y], UPPER, r_back.at[k], dev(p, x, i, c))
        arrived_kib(6 * B4, r_f2.at[k])
        for slot, ox, c_ in ((2, 6, 0), (5, 2, 1), (0, 7, 0), (1, 7, 1), (3, 1, 0), (4, 1, 1)):
            x_ = (x + ox) % 8
            v, i = landing(k, x_, c_)
            acc = pb[k, :, v, i].astype(F32) + fb[k, slot].astype(F32)
            sb[k, slot] = acc.astype(BF)
            send(sb.at[k, slot], rb1.at[k, r * 4 + xh], UPPER, r_back2.at[k], dev(p, x_, y, c_))

    def to_sources(k):
        @pl.when(inner)
        def _():
            arrived_kib(5 * A8, r_back.at[k])

        @pl.when(jnp.logical_not(inner))
        def _():
            arrived_kib(4 * A8, r_back.at[k])

        for e in range(2):
            acc = ra1[k, 4 * e].astype(F32)
            for h in range(1, 4):
                acc = acc + ra1[k, 4 * e + h].astype(F32)
            for h in range(4):
                ta[k, h, e] = acc[2 * h : 2 * h + 2].astype(BF)
        r_ = (k + 8 - y) % 4
        for h in range(4):
            send(ta.at[k, h], ra2.at[r * 4 + xh], UPPER, r_ra2, (down, r_, y * 4 + h))
        arrived_kib(9 * B4, r_back2.at[k])
        for q in range(4):
            acc = rb1[k, 4 * q].astype(F32)
            for h in range(1, 4):
                acc = acc + rb1[k, 4 * q + h].astype(F32)
            for h in range(2):
                tb[k, h, :, q * HB : (q + 1) * HB] = acc[h].astype(BF)
        v = (k + 4 - r) % 4
        for h in range(2):

            def go(h=h):
                send(tb.at[k, h], rb2.at[y], UPPER, r_rb2, dev(p, x, v + 4 * h, c))

            pl.when(v + 4 * h != y)(go)

            @pl.when(v + 4 * h == y)
            def _(h=h):
                rb2[y] = tb[k, h]

    def mixed(e, base, m, back):
        for f in range(2):
            for h in range(2):
                base = base + m[2 * e : 2 * e + 2, 2 * f + h : 2 * f + h + 1] * back[f][h : h + 1, :]
        return base.astype(BF)

    def next_rows():
        @pl.when(upper)
        def _():
            arrived(rb2.at[0:7], r_rb2)
            back = []
            for f in range(2):
                acc = rb2[4 * f].astype(F32)
                for h in range(1, 4):
                    acc = acc + rb2[4 * f + h].astype(F32)
                back.append(acc)
            for q in range(4):
                for e in range(2):
                    rows_b[1, e, :, q * HB : (q + 1) * HB] = mixed(
                        e,
                        base_v[2 * e : 2 * e + 2, q * Q + HA : (q + 1) * Q],
                        m_v[...],
                        [b[:, q * HB : (q + 1) * HB] for b in back],
                    )
            first_b(1)

        @pl.when(lower)
        def _():
            arrived(ra2, r_ra2)
            for q in range(4):
                back = []
                for f in range(2):
                    acc = ra2[4 * q, f].astype(F32)
                    for h in range(1, 4):
                        acc = acc + ra2[4 * q + h, f].astype(F32)
                    back.append(acc)
                for e in range(2):
                    rows_a[1, q, e] = mixed(e, base_in[q, e], m_in[...], back)
            first_a(1)

    def gather_rows(k):
        pl.when(mine == k)(next_rows)

    for k in range(K):
        dispatched(0, k)
        pl.when(upper)(functools.partial(hidden_gradient, k))
    for k in range(K):
        pl.when(upper)(functools.partial(input_gradient, k))
    left = jnp.concatenate([avt[0, k] for k in range(K)], axis=1)
    out[0, :, 0:HA] = dot(left, ha[0].reshape(K * 64, HA), ((1,), (0,)))
    out[0, :, HA:Q] = dot(left, hd[0].reshape(K * 64, HB), ((1,), (0,)))
    for k in range(K):
        pl.when(upper)(functools.partial(forward_back, k))
    arrived(av1.at[0:3], r_one.at[4])
    for k in range(K):
        av = jnp.concatenate([av1[(k - yy) % 4, 8 * yy : 8 * yy + 8] for yy in range(8)], axis=0)
        avt[1, k] = av.astype(F32).T.astype(BF)

    @pl.when(lower)
    def _():
        arrived(base_in, r_one.at[2])
        arrived(m_in, r_one.at[3])

    def if_lower(step, *args):
        pl.when(lower)(functools.partial(step, *args))

    def finish(k):
        dispatched(1, k)
        out[0, :, 0:HA] += dot(avt[1, k], ha[1, k].reshape(64, HA), ((1,), (0,)))
        out[0, :, HA:Q] += dot(avt[1, k], hd[1, k], ((1,), (0,)))

    pl.when(upper)(functools.partial(to_sources, 0))
    pl.when(upper)(functools.partial(to_sources, 1))
    pl.when(upper)(functools.partial(to_sources, 2))
    pl.when(upper)(functools.partial(to_sources, 3))
    gather_rows(0)
    gather_rows(1)
    gather_rows(2)
    gather_rows(3)
    if_lower(second, 1, 0)
    if_lower(second, 1, 1)
    if_lower(second, 1, 2)
    if_lower(second, 1, 3)
    if_lower(forward, 1, 0)
    if_lower(forward, 1, 1)
    if_lower(forward, 1, 2)
    if_lower(forward, 1, 3)
    for k in range(K):
        if_lower(finish, k)

    def second_size(forwards):
        return 16 * A8 + K * forwards * A8 + 60 * B4

    first_a_size, first_b_size = 15 * B4, 7 * ROWS2
    all_size = first_a_size + first_b_size + 3 * UV128 + 3 * DX64
    for chosen, forwards in ((inner, 4), (jnp.logical_not(inner), 2)):
        @pl.when(chosen)
        def _(forwards=forwards):
            arrived_kib(all_size + second_size(forwards), snd.at[ALL])

        @pl.when(chosen & lower)
        def _(forwards=forwards):
            arrived_kib(first_a_size + second_size(forwards), snd.at[LOWER])

    @pl.when(lower)
    def _():
        arrived(sel_in, snd.at[SEL])

    @pl.when(upper)
    def _():
        arrived_kib(8 * ROWS2 + 12 * DX64 + 28 * A8 + 60 * B4 + 16 * B4 + 7 * ROWS2 + 56, snd.at[UPPER])
        arrived(m_in, snd.at[MM])


def body(cotangent, routes, gates, *others):
    hbm = pl.BlockSpec(memory_space=pl.ANY)
    dma = pltpu.SemaphoreType.DMA
    vmem = pltpu.VMEM
    return pl.pallas_call(
        kernel,
        out_shape=vmem((1, HID, Q), F32),
        in_specs=[hbm] * 8,
        out_specs=pl.BlockSpec(memory_space=vmem),
        scratch_shapes=[
            vmem((TOK, D), BF),
            vmem((2, 8, TOK), jnp.int32),
            vmem((2, 8, TOK), BF),
            vmem((HID, Q), BF),
            vmem((Q, 2 * HID), BF),
            vmem((Q, HID), BF),
            vmem((2 * HID, Q), BF),
            vmem((3, 8, TOK), BF),
            vmem((8, TOK), BF),
            vmem((2, 4, 2, 2, HA), BF),
            vmem((2, 2, 2, 4 * HB), BF),
            vmem((8, D), F32),
            vmem((4, 2, 2, HA), F32),
            vmem((4, 2, 2, HA), F32),
            vmem((8, 8), F32),
            vmem((8, 8), F32),
            vmem((4, 2, 32, 2, HID), BF),
            vmem((2, 32, 2, HID), BF),
            vmem((4, TOK, HID), BF),
            vmem((K, 2, 64, HID), F32),
            vmem((2, K, HID, 64), BF),
            vmem((1536, 4, 128), BF),
            vmem((2, K, 4, 2, 2, HA), BF),
            vmem((2, K, 2, 8, HA), BF),
            vmem((2, 4, 2, 2, 4 * HB), BF),
            vmem((2, K, 8, 8, HA), BF),
            vmem((2, K, 2, 4, 4, 2, HB), BF),
            vmem((2, K, 64, HB), BF),
            vmem((K, 4, 64, HID), BF),
            vmem((K, 8, 8, HA), BF),
            vmem((K, 2, 4, 4, 2, HB), BF),
            vmem((K, 3, 8, HA), BF),
            vmem((K, 6, 2, 2, HB), BF),
            vmem((K, 2, 8, HA), BF),
            vmem((K, 6, 2, 2, HB), BF),
            vmem((K, 8, 8, HA), BF),
            vmem((K, 16, 2, 2, HB), BF),
            vmem((K, 4, 2, 2, HA), BF),
            vmem((K, 2, 2, 4 * HB), BF),
            vmem((16, 2, 2, HA), BF),
            vmem((8, 2, 4 * HB), BF),
            dma((5,)),
            dma((5,)),
            dma((2, K)),
            dma((2, K)),
            dma((2, K)),
            dma((K,)),
            dma((K,)),
            dma((K,)),
            dma,
            dma,
            dma((5,)),
            pltpu.SemaphoreType.REGULAR,
            dma((2, K)),
            dma((2, K)),
            dma((K,)),
            dma((K,)),
        ],
        compiler_params=pltpu.CompilerParams(collective_id=0, has_side_effects=True),
        name="cooldown",
    )(cotangent, jnp.swapaxes(routes, 2, 3), jnp.swapaxes(gates, 2, 3), *others)


def solution(mesh):
    in_specs = (
        P("pipe", ("dp", "expert"), None),
        P("pipe", None, ("dp", "expert"), None),
        P("pipe", None, ("dp", "expert"), None),
        P("pipe", None, "dp", None, None, "expert"),
        P("pipe", None, "dp", None, None, "expert"),
        P("pipe", None, "expert"),
        P("pipe", None, "expert"),
        P("pipe", "expert", None),
    )
    out_specs = P("pipe", "expert", "dp")
    return jax.shard_map(body, mesh=mesh, in_specs=in_specs, out_specs=out_specs, check_vma=False)
```

time: 62.6 us -> 62.4 us (level)
  the two profiles are of different devices: /device:TPU:384 before, /device:TPU:387 now
where the time goes in v5:
time: 62.4 us; the launch traced here: 62.2 us
  Pallas kernels  61.3 us (98%)
  local copies, waits for them, and re-layouts  0.93 us (1%)
    pallas_call x1, Pallas kernels, body(): pl.pallas_call(kernel, out_shape=vmem((1, HID, Q), F32), in_specs=[hbm] *...  61.3 us

profile of v5, /device:TPU:387, one launch (start us, length us, event | category | flops | bytes accessed | tf_op | source)
XLA Modules:
  0.0 62.2 jit_solution(2201455014368018285)
XLA Ops:
  0.0 61.3 %cooldown.1 = f32[1,128,1792]{2,1,0:T(8,128)S(1)} custom-call(bf16[1,64,7168]{2,1,0:T(8,128)(2,1)} %cot.1, s32[1,2,8,64]{3,2,1,0:T(8,128)} %bitcast.2, bf16[1,2,8,64]{3,2,1,0:T(8,128)(2,1)} %bitcast.3, bf16[1,2,1,32,2,128]{5,4,3,2,1,0:T(2,128)(2,1)} %gate_pre.1, bf16[1,2,1,32,2,128]{5,4,3,2,1,0:T(2,128)(2,1)} %up_pre.1, bf16[1,7168,128]{2,1,0:T(8,128)(2,1)} %w_gate.1, ...), custom_call_target="tpu_custom_call" | custom-call | tf_op jit(solution)/shard_map/cooldown/pallas_call | solution.py:517
  61.3 0.9 %copy.10 = f32[1,128,1792]{2,1,0:T(8,128)} copy(f32[1,128,1792]{2,1,0:T(8,128)S(1)} %cooldown.1) | data formatting | bytes 1835008

commit v6 on v5

--- a/solution.py
+++ b/solution.py
@@ -237,7 +237,7 @@
         arrived_kib(3 * A8 + 6 * B4, r_far.at[t, k])
         hd[t, k] = hb[t, k].reshape(64, HB)
 
-    others = [(ol, oc) for ol in (0, 1) for oc in (0, 1) if (ol, oc) != (0, 0)]
+    others = ((1, 0), (1, 1), (0, 1))
 
     def peer(ol, oc):
         return ((r // 2 + ol) % 2) * 2 + (c + oc) % 2
@@ -375,8 +375,10 @@
             for h in range(4):
                 ta[k, h, e] = acc[2 * h : 2 * h + 2].astype(BF)
         r_ = (k + 8 - y) % 4
-        for h in range(4):
-            send(ta.at[k, h], ra2.at[r * 4 + xh], UPPER, r_ra2, (down, r_, y * 4 + h))
+        side = 1 + 2 * (x % 2)
+        for o in (2, side, 4 - side, 0):
+            h_ = (xh + o) % 4
+            send(ta.at[k, h_], ra2.at[r * 4 + xh], UPPER, r_ra2, (down, r_, y * 4 + h_))
         arrived_kib(9 * B4, r_back2.at[k])
         for q in range(4):
             acc = rb1[k, 4 * q].astype(F32)
@@ -385,14 +387,17 @@
             for h in range(2):
                 tb[k, h, :, q * HB : (q + 1) * HB] = acc[h].astype(BF)
         v = (k + 4 - r) % 4
-        for h in range(2):
-
-            def go(h=h):
-                send(tb.at[k, h], rb2.at[y], UPPER, r_rb2, dev(p, x, v + 4 * h, c))
-
-            pl.when(v + 4 * h != y)(go)
-
-            @pl.when(v + 4 * h == y)
+        d = (v + 8 - y) % 4
+        far = (y + jnp.where(d < 2, d + 4, d)) % 8 // 4
+        for h in (far, 1 - far):
+            y_ = v + 4 * h
+
+            def go(h=h, y_=y_):
+                send(tb.at[k, h], rb2.at[y], UPPER, r_rb2, dev(p, x, y_, c))
+
+            pl.when(y_ != y)(go)
+
+            @pl.when(y_ == y)
             def _(h=h):
                 rb2[y] = tb[k, h]
 

time: 62.4 us -> 62.1 us (level)
  the two profiles are of different devices: /device:TPU:387 before, /device:TPU:1 now
where the time goes in v6:
time: 62.1 us; the launch traced here: 61.2 us
  Pallas kernels  60.2 us (97%)
  local copies, waits for them, and re-layouts  0.93 us (1%)
    pallas_call x1, Pallas kernels, body(): pl.pallas_call(kernel, out_shape=vmem((1, HID, Q), F32), in_specs=[hbm] *...  60.2 us

profile of v6, /device:TPU:1, one launch (start us, length us, event | category | flops | bytes accessed | tf_op | source)
XLA Modules:
  0.0 61.2 jit_solution(12300559648919219304)
XLA Ops:
  0.0 60.2 %cooldown.1 = f32[1,128,1792]{2,1,0:T(8,128)S(1)} custom-call(bf16[1,64,7168]{2,1,0:T(8,128)(2,1)} %cot.1, s32[1,2,8,64]{3,2,1,0:T(8,128)} %bitcast.2, bf16[1,2,8,64]{3,2,1,0:T(8,128)(2,1)} %bitcast.3, bf16[1,2,1,32,2,128]{5,4,3,2,1,0:T(2,128)(2,1)} %gate_pre.1, bf16[1,2,1,32,2,128]{5,4,3,2,1,0:T(2,128)(2,1)} %up_pre.1, bf16[1,7168,128]{2,1,0:T(8,128)(2,1)} %w_gate.1, ...), custom_call_target="tpu_custom_call" | custom-call | tf_op jit(solution)/shard_map/cooldown/pallas_call | solution.py:522
  60.3 0.9 %copy.10 = f32[1,128,1792]{2,1,0:T(8,128)} copy(f32[1,128,1792]{2,1,0:T(8,128)S(1)} %cooldown.1) | data formatting | bytes 1835008

commit v7 on v6

--- a/solution.py
+++ b/solution.py
@@ -251,20 +251,21 @@
     av1[r] = (u * jax.nn.sigmoid(u) * v).astype(BF)
     for ol, oc in others:
         send(av1.at[r], av1.at[r], ALL, r_one.at[4], (p, peer(ol, oc), s))
-    @pl.when(lower & upper)
-    def _():
-        pl.semaphore_wait(ready, 1)
-
-    @pl.when(lower)
-    def _():
-        send(sel_s.at[2], sel_in, SEL, r_one.at[0], dev(up, x, y, c))
-
-    for k in range(K):
-        second(0, k)
-
     arrived_kib(3 * Q // 4, ld.at[3])
     w2t[...] = w2[...].astype(F32).T.astype(BF)
     w13t[...] = w13[...].astype(F32).T.astype(BF)
+
+    @pl.when(lower & upper)
+    def _():
+        pl.semaphore_wait(ready, 1)
+
+    @pl.when(lower)
+    def _():
+        send(sel_s.at[2], sel_in, SEL, r_one.at[0], dev(up, x, y, c))
+
+    for k in range(K):
+        second(0, k)
+
     for k in range(K):
         forward(0, k)
 

time: 62.1 us -> 62.1 us (level)
  no operation moved by 1% of the time
where the time goes in v7:
time: 62.1 us; the launch traced here: 61.2 us
  Pallas kernels  60.2 us (97%)
  local copies, waits for them, and re-layouts  0.93 us (1%)
    pallas_call x1, Pallas kernels, body(): pl.pallas_call(kernel, out_shape=vmem((1, HID, Q), F32), in_specs=[hbm] *...  60.2 us

profile of v7, /device:TPU:1, one launch (start us, length us, event | category | flops | bytes accessed | tf_op | source)
XLA Modules:
  0.0 61.2 jit_solution(4152243913485280556)
XLA Ops:
  0.0 60.2 %cooldown.1 = f32[1,128,1792]{2,1,0:T(8,128)S(1)} custom-call(bf16[1,64,7168]{2,1,0:T(8,128)(2,1)} %cot.1, s32[1,2,8,64]{3,2,1,0:T(8,128)} %bitcast.2, bf16[1,2,8,64]{3,2,1,0:T(8,128)(2,1)} %bitcast.3, bf16[1,2,1,32,2,128]{5,4,3,2,1,0:T(2,128)(2,1)} %gate_pre.1, bf16[1,2,1,32,2,128]{5,4,3,2,1,0:T(2,128)(2,1)} %up_pre.1, bf16[1,7168,128]{2,1,0:T(8,128)(2,1)} %w_gate.1, ...), custom_call_target="tpu_custom_call" | custom-call | tf_op jit(solution)/shard_map/cooldown/pallas_call | solution.py:523
  60.3 0.9 %copy.10 = f32[1,128,1792]{2,1,0:T(8,128)} copy(f32[1,128,1792]{2,1,0:T(8,128)S(1)} %cooldown.1) | data formatting | bytes 1835008

commit v8 on v5

--- a/solution.py
+++ b/solution.py
@@ -62,6 +62,13 @@
     def arrived(like, sem):
         pltpu.make_async_copy(like, like, sem).wait()
 
+    def each_chunk(step):
+        def turn_of(k, carry):
+            step(k)
+            return carry
+
+        lax.fori_loop(0, K, turn_of, 0)
+
     def arrived_kib(size, sem):
         arrived(void.at[0:size], sem)
 
@@ -259,14 +266,11 @@
     def _():
         send(sel_s.at[2], sel_in, SEL, r_one.at[0], dev(up, x, y, c))
 
-    for k in range(K):
-        second(0, k)
-
+    each_chunk(functools.partial(second, 0))
     arrived_kib(3 * Q // 4, ld.at[3])
     w2t[...] = w2[...].astype(F32).T.astype(BF)
     w13t[...] = w13[...].astype(F32).T.astype(BF)
-    for k in range(K):
-        forward(0, k)
+    each_chunk(functools.partial(forward, 0))
 
     @pl.when(upper)
     def _():
@@ -436,19 +440,16 @@
                     rows_a[1, q, e] = mixed(e, base_in[q, e], m_in[...], back)
             first_a(1)
 
-    def gather_rows(k):
-        pl.when(mine == k)(next_rows)
-
-    for k in range(K):
+    def to_hidden(k):
         dispatched(0, k)
         pl.when(upper)(functools.partial(hidden_gradient, k))
-    for k in range(K):
-        pl.when(upper)(functools.partial(input_gradient, k))
+
+    each_chunk(to_hidden)
+    pl.when(upper)(functools.partial(each_chunk, input_gradient))
     left = jnp.concatenate([avt[0, k] for k in range(K)], axis=1)
     out[0, :, 0:HA] = dot(left, ha[0].reshape(K * 64, HA), ((1,), (0,)))
     out[0, :, HA:Q] = dot(left, hd[0].reshape(K * 64, HB), ((1,), (0,)))
-    for k in range(K):
-        pl.when(upper)(functools.partial(forward_back, k))
+    pl.when(upper)(functools.partial(each_chunk, forward_back))
     arrived(av1.at[0:3], r_one.at[4])
     for k in range(K):
         av = jnp.concatenate([av1[(k - yy) % 4, 8 * yy : 8 * yy + 8] for yy in range(8)], axis=0)
@@ -459,32 +460,19 @@
         arrived(base_in, r_one.at[2])
         arrived(m_in, r_one.at[3])
 
-    def if_lower(step, *args):
-        pl.when(lower)(functools.partial(step, *args))
-
     def finish(k):
         dispatched(1, k)
         out[0, :, 0:HA] += dot(avt[1, k], ha[1, k].reshape(64, HA), ((1,), (0,)))
         out[0, :, HA:Q] += dot(avt[1, k], hd[1, k], ((1,), (0,)))
 
-    pl.when(upper)(functools.partial(to_sources, 0))
-    pl.when(upper)(functools.partial(to_sources, 1))
-    pl.when(upper)(functools.partial(to_sources, 2))
-    pl.when(upper)(functools.partial(to_sources, 3))
-    gather_rows(0)
-    gather_rows(1)
-    gather_rows(2)
-    gather_rows(3)
-    if_lower(second, 1, 0)
-    if_lower(second, 1, 1)
-    if_lower(second, 1, 2)
-    if_lower(second, 1, 3)
-    if_lower(forward, 1, 0)
-    if_lower(forward, 1, 1)
-    if_lower(forward, 1, 2)
-    if_lower(forward, 1, 3)
-    for k in range(K):
-        if_lower(finish, k)
+    pl.when(upper)(functools.partial(each_chunk, to_sources))
+    next_rows()
+
+    @pl.when(lower)
+    def _():
+        each_chunk(functools.partial(second, 1))
+        each_chunk(functools.partial(forward, 1))
+        each_chunk(finish)
 
     def second_size(forwards):
         return 16 * A8 + K * forwards * A8 + 60 * B4

time: 62.4 us -> 62.3 us (level)
  the two profiles are of different devices: /device:TPU:387 before, /device:TPU:384 now
where the time goes in v8:
time: 62.3 us; the launch traced here: 62.2 us
  Pallas kernels  61.2 us (98%)
  local copies, waits for them, and re-layouts  0.93 us (1%)
    pallas_call x1, Pallas kernels, body(): pl.pallas_call(kernel, out_shape=vmem((1, HID, Q), F32), in_specs=[hbm] *...  61.2 us

profile of v8, /device:TPU:384, one launch (start us, length us, event | category | flops | bytes accessed | tf_op | source)
XLA Modules:
  0.0 62.2 jit_solution(15923145320533934905)
XLA Ops:
  0.0 61.2 %cooldown.1 = f32[1,128,1792]{2,1,0:T(8,128)S(1)} custom-call(bf16[1,64,7168]{2,1,0:T(8,128)(2,1)} %cot.1, s32[1,2,8,64]{3,2,1,0:T(8,128)} %bitcast.2, bf16[1,2,8,64]{3,2,1,0:T(8,128)(2,1)} %bitcast.3, bf16[1,2,1,32,2,128]{5,4,3,2,1,0:T(2,128)(2,1)} %gate_pre.1, bf16[1,2,1,32,2,128]{5,4,3,2,1,0:T(2,128)(2,1)} %up_pre.1, bf16[1,7168,128]{2,1,0:T(8,128)(2,1)} %w_gate.1, ...), custom_call_target="tpu_custom_call" | custom-call | tf_op jit(solution)/shard_map/cooldown/pallas_call | solution.py:505
  61.2 0.9 %copy.10 = f32[1,128,1792]{2,1,0:T(8,128)} copy(f32[1,128,1792]{2,1,0:T(8,128)S(1)} %cooldown.1) | data formatting | bytes 1835008
